TPU v7x, 32 devices: a 4x4x1 block of a 4x4x8 slice. The times are simulated.
32 devices in a mesh: dp: 1 (over z), tp: 4 (over y), sp: 8 (over x, core).
Axes of the slice: x: 4, y: 4, z: 1, core: 2. Of those that a mesh axis runs over, the one named last changes fastest.
The devices are a block of a 4x4x8 slice.
Arguments:
- hidden: bfloat16 [64, 8192], P('dp')
- norm_scale: bfloat16 [8192], replicated
- w_qkv: bfloat16 [8192, 10240], P(None, 'tp')
- w_out: bfloat16 [8192, 8192], P('tp')
- k_cache: bfloat16 [64, 1024, 8, 128], P('dp', 'sp', 'tp')
- v_cache: bfloat16 [64, 1024, 8, 128], P('dp', 'sp', 'tp')
- positions: int32 [64], P('dp')
Outputs:
- output 1: bfloat16 [64, 8192], P('dp')
- output 2: bfloat16 [64, 1024, 8, 128], P('dp', 'sp', 'tp')
- output 3: bfloat16 [64, 1024, 8, 128], P('dp', 'sp', 'tp')
All inputs are finite; a program needn't handle non-finite values.
Results may differ from a plain program's by a relative error of at most 0.00668127.
Values sent between devices are 32-bit elements.
A program may use at most 768 MiB of HBM per device.

v0:
```python
import math
import jax
import jax.numpy as jnp
from jax import lax
from jax.sharding import PartitionSpec as P


def rope_apply(head_vals, positions):
    half_dim = head_vals.shape[-1] // 2
    inv_freq = jnp.exp(jnp.arange(half_dim, dtype=jnp.float32) * (-2.0 * math.log(500000.0) / head_vals.shape[-1]))
    angles = positions.astype(jnp.float32)[:, None] * inv_freq[None, :]
    cos_part = jnp.cos(angles)[:, None, None, :]
    sin_part = jnp.sin(angles)[:, None, None, :]
    first_half = head_vals[..., :half_dim]
    second_half = head_vals[..., half_dim:]
    return jnp.concatenate([first_half * cos_part - second_half * sin_part, second_half * cos_part + first_half * sin_part], axis=-1)


def layer_norm_bf16(hidden_f32, norm_scale):
    row_mean = jnp.mean(hidden_f32, axis=-1, keepdims=True)
    centered = hidden_f32 - row_mean
    row_var = jnp.mean(centered * centered, axis=-1, keepdims=True)
    return (centered * lax.rsqrt(row_var + 1e-5) * norm_scale.astype(jnp.float32)).astype(jnp.bfloat16)


def solution(mesh):
    cache_spec = P('dp', 'sp', 'tp', None)

    def local_step(hidden, norm_scale, w_qkv, w_out, k_cache, v_cache, positions):
        n_seq, seq_local, kv_local, head_dim = k_cache.shape
        q_per_kv = w_qkv.shape[1] // (kv_local * head_dim) - 2
        hidden_f32 = hidden.astype(jnp.float32)
        normed = layer_norm_bf16(hidden_f32, norm_scale)
        qkv_proj = jnp.clip(jnp.dot(normed, w_qkv, preferred_element_type=jnp.float32).astype(jnp.bfloat16), -8.0, 8.0)
        grouped = qkv_proj.reshape(n_seq, kv_local, q_per_kv + 2, head_dim)
        rotated = rope_apply(grouped[:, :, : q_per_kv + 1].astype(jnp.float32), positions).astype(jnp.bfloat16)
        queries = rotated[:, :, :q_per_kv]
        row_index = lax.axis_index('sp') * seq_local + jnp.arange(seq_local)
        new_row = (row_index[None, :] == positions[:, None])[:, :, None, None]
        k_upd = jnp.where(new_row, rotated[:, :, q_per_kv][:, None], k_cache)
        v_upd = jnp.where(new_row, grouped[:, :, q_per_kv + 1][:, None], v_cache)
        scores = jnp.einsum('bgqd,bsgd->bgqs', queries, k_upd, preferred_element_type=jnp.float32) * (head_dim ** -0.5)
        valid_mask = row_index[None, :] <= positions[:, None]
        scores = jnp.where(valid_mask[:, None, None, :], scores, -1e30)
        local_max = jnp.max(scores, axis=-1)
        weights = jnp.exp(scores - local_max[..., None])
        local_sum = jnp.sum(weights, axis=-1)
        local_out = jnp.einsum('bgqs,bsgd->bgqd', weights.astype(jnp.bfloat16), v_upd, preferred_element_type=jnp.float32)
        global_max = lax.pmax(local_max, 'sp')
        factor = jnp.exp(local_max - global_max)
        packed = jnp.concatenate([local_out * factor[..., None], (local_sum * factor)[..., None]], axis=-1)
        merged = lax.psum(packed, 'sp')
        attn_out = merged[..., :head_dim] / merged[..., head_dim:]
        attn_flat = attn_out.reshape(n_seq, kv_local * q_per_kv * head_dim).astype(jnp.bfloat16)
        head_part = jnp.dot(attn_flat, w_out, preferred_element_type=jnp.float32)
        proj_sum = lax.psum(head_part, 'tp')
        h_out = (hidden_f32 + proj_sum).astype(jnp.bfloat16)
        return h_out, k_upd, v_upd

    return jax.shard_map(
        local_step,
        mesh=mesh,
        in_specs=(P('dp', None), P(None), P(None, 'tp'), P('tp', None), cache_spec, cache_spec, P('dp')),
        out_specs=(P('dp', None), cache_spec, cache_spec),
        check_vma=False,
    )
```

profile of v0, /device:TPU:97, one launch (start us, length us, event | category | flops | bytes accessed | tf_op | source)
XLA Modules:
  0.0 220.1 jit_solution(13706386330794658575)
XLA Ops:
  7.2 0.1 all-reduce.3.cloned.1.call-start
  7.3 1.5 convert_reduce_fusion
  8.7 1.7 fusion.7
  10.4 0.7 convert_element_type.36
  11.2 0.0 copy-start.3
  11.2 17.1 %fusion.4 = bf16[64,2560]{1,0:T(8,128)(2,1)S(1)} fusion(bf16[8192,2560]{1,0:T(8,128)(2,1)} %param.9, bf16[64,8192]{1,0:T(8,128)(2,1)} %param.7, f32[8192]{0:T(1024)S(1)} %convert_element_type.36, f32[64]{0:T(128)S(1)} %add_rsqrt_fusion, f32[64]{0:T(128)S(1)} %broadcast_multiply_fusion), kind=kOutput, calls=%fused_computation.7 | convolution fusion | flops 2687303680 | bytes 43352576 | tf_op jit(solution)/shard_map/dot_general | solution.py:34
  28.3 0.2 reshape.131
  28.5 0.1 slice.37
  28.5 0.1 slice_convert_fusion
  28.7 0.0 copy-start.2
  28.7 0.0 copy-done.3
  28.7 0.1 broadcast_compare_fusion.1
  28.9 0.2 multiply_cosine_fusion
  29.1 0.5 subtract_convert_fusion
  29.6 0.2 pad_maximum_fusion.1
  29.9 1.0 copy-done.2
  30.9 13.5 %broadcast_select_fusion = (bf16[64,128,2,128]{3,2,1,0:T(2,128)(2,1)}, bf16[64,128,2,128]{3,2,1,0:T(2,128)(2,1)S(1)}) fusion(bf16[64,128,2,128]{3,2,1,0:T(2,128)(2,1)S(1)} %copy-done.2, pred[64,128]{1,0:T(8,128)(4,1)S(1)} %get-tuple-element.10, bf16[64,2,128]{2,1,0:T(2,128)(2,1)S(1)} %copy.27, bf16[64,128,2,128]{3,2,1,0:T(2,128)(2,1)} %param.11, ...), kind=kLoop, calls=%fused_computation | loop fusion | flops 4194304 | bytes 16850944 | tf_op jit(solution)/shard_map/jit(_where)/select_n | solution.py:41
  44.4 0.0 copy-start.1
  44.4 2.0 copy-done.1
  46.4 2.4 %fusion.35 = (f32[64,2,8]{2,1,0:T(2,128)S(1)}, f32[64,2,8,128]{3,2,1,0:T(8,128)S(1)}) fusion(bf16[64,128,2,128]{3,2,1,0:T(2,128)(2,1)S(1)} %get-tuple-element.8, bf16[64,2,9,64]{3,2,1,0:T(8,128)(2,1)S(1)} %get-tuple-element.5, bf16[64,2,9,64]{3,2,1,0:T(8,128)(2,1)S(1)} %get-tuple-element.6, pred[64,128]{1,0:T(8,128)(4,1)S(1)} %get-tuple-element.9), kind=kOutput, calls=%fused_computation.53 | convolution fusion | flops 34470912 | bytes 5025792 | tf_op jit(solution)/shard_map/bgqd,bsgd->bgqs/dot_general | solution.py:42
  48.9 24.5 %pmax.7 = f32[64,2,8]{2,1,0:T(2,128)S(1)} all-reduce(f32[64,2,8]{2,1,0:T(2,128)S(1)} %get-tuple-element.13), channel_id=1, replica_groups=mesh['dp'=1,'tp'=4,'sp'=8] {'sp'}, use_global_device_ids=true, to_apply=%region_3.4 | all-reduce | flops 1024 | bytes 8192 | tf_op jit(solution)/shard_map/pmax | solution.py:49
  73.4 0.4 fusion.25
  73.8 0.1 multiply_bitcast_fusion
  73.9 0.8 copy.30
  74.7 3.4 %fusion.17 = f32[64,2,8,128]{3,2,1,0:T(8,128)S(1)} fusion(bf16[64,128,2,128]{3,2,1,0:T(2,128)(2,1)} %get-tuple-element.7, f32[64,2,8,128]{3,2,1,0:T(8,128)S(1)} %get-tuple-element.14, f32[64,2,8]{2,1,0:T(2,128)S(1)} %get-tuple-element.4, f32[64,2,8]{2,1,0:T(2,128)S(1)} %get-tuple-element.13), kind=kOutput, calls=%fused_computation.19 | convolution fusion | flops 33947648 | bytes 5251072 | tf_op jit(solution)/shard_map/bgqs,bsgd->bgqd/dot_general | solution.py:48
  78.1 1.1 pad_maximum_fusion
  79.2 0.1 all-reduce.3.cloned.1.call-update
  79.3 0.2 all-reduce.5.cloned.1.call-start
  79.5 58.6 %all-reduce.3.cloned.1.call-done = f32[64,2,8,129]{3,2,1,0:T(8,128)} async-done(((f32[64,2,8,129]{3,2,1,0:T(8,128)}), f32[64,2,8,129]{3,2,1,0:T(8,128)}) %all-reduce.3.cloned.1.call-update) | async-done | bytes 528400 | tf_op jit(solution)/shard_map/psum | solution.py:52
  138.1 1.1 slice.39
  139.2 0.3 copy.31
  139.4 0.1 copy.32
  139.5 1.3 fusion.24
  140.8 0.0 copy-start
  140.8 15.0 %fusion.30 = f32[64,8192]{1,0:T(8,128)} fusion(bf16[2048,8192]{1,0:T(8,128)(2,1)} %param.10, bf16[8,8,16,128]{3,2,1,0:T(8,128)(2,1)S(1)} %bitcast.16), kind=kOutput, calls=%fused_computation.35 | convolution fusion | flops 2147483648 | bytes 35913728 | tf_op jit(solution)/shard_map/dot_general | solution.py:55
  155.8 0.1 all-reduce.5.cloned.1.call-update
  155.8 54.7 %all-reduce.5.cloned.1.call-done = f32[64,8192]{1,0:T(8,128)} async-done(((f32[64,8192]{1,0:T(8,128)}), f32[64,8192]{1,0:T(8,128)}) %all-reduce.5.cloned.1.call-update) | async-done | bytes 2097168 | tf_op jit(solution)/shard_map/psum | solution.py:56
  210.5 0.0 copy-done
  210.5 2.7 %fusion.10 = bf16[64,8192]{1,0:T(8,128)(2,1)} fusion(f32[64,8192]{1,0:T(8,128)} %all-reduce.5.cloned.1.call-done, bf16[64,8192]{1,0:T(8,128)(2,1)S(1)} %copy-done), kind=kLoop, calls=%fused_computation.16 | loop fusion | flops 1572864 | bytes 4194304 | tf_op jit(solution)/shard_map/convert_element_type | solution.py:57
  (9 shorter events, 0.1 us)
Async XLA Ops:
  7.2 130.9 %all-reduce.3.cloned.1.call-start = ((), (), s32[]{:S(2)}) async-start(), calls=%async_computation | async-start | bytes 2097152 | tf_op jit(solution)/shard_map/psum | solution.py:52
  11.2 17.6 %copy-start.3 = (s32[64]{0:T(128)S(1)}, s32[64]{0:T(128)}, u32[]{:S(2)}) copy-start(s32[64]{0:T(128)} %param.13) | copy-start | bytes 772
  28.7 2.2 copy-start.2
  44.4 2.0 copy-start.1
  79.3 131.3 %all-reduce.5.cloned.1.call-start = ((), (), s32[]{:S(2)}) async-start(), calls=%async_computation.1 | async-start | bytes 4194304 | tf_op jit(solution)/shard_map/psum | solution.py:56
  140.8 69.7 %copy-start = (bf16[64,8192]{1,0:T(8,128)(2,1)S(1)}, bf16[64,8192]{1,0:T(8,128)(2,1)}, u32[]{:S(2)}) copy-start(bf16[64,8192]{1,0:T(8,128)(2,1)} %param.7) | copy-start | bytes 3145732
Sparse Core Ops, SparseCore 0:
  79.4 58.6 all-reduce.2
  156.0 54.5 all-reduce.4
where the time goes:
time: 221 us; the launch traced here: 220 us
  waiting for transfers between devices  113 us (51%)
  matrix products  37.9 us (17%)
  blocking collectives  24.5 us (11%)
  other arithmetic  24.1 us (11%)
  between operations  14.3 us (6%)
  local copies, waits for them, and re-layouts  5.68 us (3%)
    psum x1, waiting for transfers between devices, local_step(): merged = lax.psum(packed, 'sp')  58.6 us
    psum x1, waiting for transfers between devices, local_step(): proj_sum = lax.psum(head_part, 'tp')  54.7 us
    pmax x1, blocking collectives, local_step(): global_max = lax.pmax(local_max, 'sp')  24.5 us
    dot_general x1, matrix products, local_step(): jnp.dot(normed, w_qkv, preferred_element_type=jnp.float32)  17.1 us
    dot_general x1, matrix products, local_step(): head_part = jnp.dot(attn_flat, w_out, preferred_element_type=jnp.float32)  15 us
    select_n x1, other arithmetic, local_step(): v_upd = jnp.where(new_row, grouped[:, :, q_per_kv + 1][:, None], v_cache)  13.5 us
  transfers between devices with their start and end apart: 2, of which 2 were waited for; matrix products, arithmetic and copies ran while one was open for 0% of the time, Pallas kernels for 0%

commit v1 on v0

v1 whole, which is shorter than its diff:
```python
import functools
import math

import jax
import jax.numpy as jnp
from jax import lax
from jax.experimental import pallas as pl
from jax.experimental.pallas import tpu as pltpu
from jax.sharding import PartitionSpec as P

MESH = pl.DeviceIdType.MESH
F32 = jnp.float32
BF16 = jnp.bfloat16
ANY = pl.BlockSpec(memory_space=pl.ANY)
VMEM = pl.BlockSpec(memory_space=pltpu.VMEM)
SMEM = pl.BlockSpec(memory_space=pltpu.SMEM)
CORES = 2
VMEM_LIMIT = 60 * 1024 * 1024


def ds(start, size, align):
    return pl.ds(pl.multiple_of(start, align), size)


def rcopy(src, dst, send_sem, recv_sem, **where):
    return pltpu.make_async_remote_copy(
        src_ref=src, dst_ref=dst, send_sem=send_sem, recv_sem=recv_sem,
        device_id=where, device_id_type=MESH,
    )


def qkv_kernel(dims, h_ref, scale_ref, pos_ref, w_ref, out_ref, wbuf, u_ref, acc, mine, wsem, send_sem, recv_sem):
    n_seq, d_model = h_ref.shape
    q_per_kv, head = dims
    n_blk, blk, cols = wbuf.shape
    s = lax.axis_index('sp')
    core = lax.rem(s, CORES)
    partner = s + 1 - 2 * core

    def wcopy(i):
        return pltpu.make_async_copy(
            w_ref.at[ds(i * blk, blk, blk), ds(core * cols, cols, 128)], wbuf.at[i], wsem.at[i])

    for i in range(n_blk):
        wcopy(i).start()
    barrier = pltpu.get_barrier_semaphore()
    pl.semaphore_signal(barrier, inc=1, device_id={'sp': partner}, device_id_type=MESH)

    lanes = 128
    zero = jnp.zeros((n_seq, lanes), F32)

    def add_sum(i, tot):
        return tot + h_ref[:, ds(i * lanes, lanes, lanes)].astype(F32)

    mean = jnp.sum(lax.fori_loop(0, d_model // lanes, add_sum, zero, unroll=8), axis=1, keepdims=True) / d_model

    def add_sq(i, tot):
        cent = h_ref[:, ds(i * lanes, lanes, lanes)].astype(F32) - mean
        return tot + cent * cent

    var = jnp.sum(lax.fori_loop(0, d_model // lanes, add_sq, zero, unroll=8), axis=1, keepdims=True) / d_model
    inv = lax.rsqrt(var + 1e-5)

    def norm(i, carry):
        cut = ds(i * lanes, lanes, lanes)
        cent = h_ref[:, cut].astype(F32) - mean
        u_ref[:, cut] = (cent * inv * scale_ref[:, cut].astype(F32)).astype(BF16)
        return carry

    lax.fori_loop(0, d_model // lanes, norm, 0, unroll=8)

    eye = lax.broadcasted_iota(jnp.int32, (n_seq, n_seq), 0) == lax.broadcasted_iota(jnp.int32, (n_seq, n_seq), 1)
    pos_col = jnp.sum(jnp.where(eye, pos_ref[...].astype(F32), 0.0), axis=1, keepdims=True)
    lane = lax.broadcasted_iota(jnp.int32, (n_seq, head), 1)
    half = head // 2
    inv_freq = jnp.exp(lax.rem(lane, half).astype(F32) * (-2.0 * math.log(500000.0) / head))
    angle = pos_col * inv_freq
    cos_t = jnp.cos(angle)
    sin_t = jnp.where(lane < half, -jnp.sin(angle), jnp.sin(angle))

    acc[...] = jnp.zeros_like(acc)

    def mm(i, carry):
        wcopy(i).wait()
        acc[...] += jnp.dot(u_ref[:, ds(i * blk, blk, blk)], wbuf[i], preferred_element_type=F32)
        return carry

    lax.fori_loop(0, n_blk, mm, 0)

    for j in range(q_per_kv + 2):
        val = jnp.clip(acc[:, j * head:(j + 1) * head].astype(BF16), -8.0, 8.0).astype(F32)
        if j < q_per_kv + 1:
            val = (val * cos_t + pltpu.roll(val, half, 1) * sin_t).astype(BF16).astype(F32)
        if j < q_per_kv:
            mine[pl.ds(j, n_seq, stride=q_per_kv), :] = val
        else:
            mine[pl.ds((j * n_seq), n_seq), :] = val
    pl.semaphore_wait(barrier, 1)
    give = rcopy(mine, out_ref.at[core], send_sem, recv_sem, sp=partner)
    give.start()
    out_ref[core] = mine[...]
    give.wait()


def attn_kernel(dims, pos_ref, qkv_ref, k_ref, v_ref, o_ref, ko_ref, vo_ref, kbuf, vbuf, isem, osem):
    q_per_kv, head = dims
    n_seq, rows2, _ = kbuf.shape
    n_grp = rows2 // qkv_ref.shape[0]
    groups = qkv_ref.shape[0]
    n_ch = o_ref.shape[0]
    per = n_seq // n_ch
    heads = groups * q_per_kv
    base = lax.axis_index('sp') * n_grp

    def cin(i, which):
        src, dst = ((k_ref, kbuf), (v_ref, vbuf))[which]
        return pltpu.make_async_copy(src.at[pl.ds(i * per, per)], dst.at[pl.ds(i * per, per)], isem.at[which, i])

    def cout(i, which):
        src, dst = ((kbuf, ko_ref), (vbuf, vo_ref))[which]
        return pltpu.make_async_copy(src.at[pl.ds(i * per, per)], dst.at[pl.ds(i * per, per)], osem.at[which, i])

    for i in range(n_ch):
        cin(i, 0).start()
        cin(i, 1).start()

    colj = lax.broadcasted_iota(jnp.int32, (heads, rows2), 1)
    rown = lax.broadcasted_iota(jnp.int32, (heads, rows2), 0)
    same = lax.rem(colj, groups) == rown // q_per_kv
    tile = 8 * groups
    trow = lax.broadcasted_iota(jnp.int32, (tile, head), 0)
    n_rows = per * heads
    eye = lax.broadcasted_iota(jnp.int32, (n_rows, n_rows), 0) == lax.broadcasted_iota(jnp.int32, (n_rows, n_rows), 1)
    q_rows = n_seq * q_per_kv

    def step(i, carry):
        cin(i, 0).wait()
        cin(i, 1).wait()
        scores = []
        for t in range(per):
            b = i * per + t
            rel = pos_ref[b] - base
            here = jnp.logical_and(rel >= 0, rel < n_grp)
            at = jnp.clip(rel, 0, n_grp - 1)
            start = (at // 8) * tile
            hit = jnp.logical_and(trow // groups == at % 8, here)
            for buf, off in ((kbuf, q_rows), (vbuf, q_rows + n_seq)):
                cut = ds(start, tile, tile)
                new = qkv_ref[0, pl.ds(off + b, 1), :]
                for g in range(1, groups):
                    new = jnp.where(trow % groups == g, qkv_ref[g, pl.ds(off + b, 1), :], new)
                buf[b, cut, :] = jnp.where(hit, new, buf[b, cut, :].astype(F32)).astype(BF16)
            q = jnp.concatenate([qkv_ref[g, ds(b * q_per_kv, q_per_kv, 8), :] for g in range(groups)], axis=0)
            sc = lax.dot_general(q.astype(BF16), kbuf[b], (((1,), (1,)), ((), ())), preferred_element_type=F32)
            ok = jnp.logical_and(same, colj < groups * (rel + 1))
            scores.append(jnp.where(ok, sc * (head ** -0.5), -1e30))
        sc = jnp.concatenate(scores, axis=0)
        top = jnp.max(sc, axis=1, keepdims=True)
        wt = jnp.exp(sc - top)
        tot = jnp.sum(wt, axis=1, keepdims=True)
        wt = wt.astype(BF16)
        for t in range(per):
            o_ref[i, t * heads:(t + 1) * heads, :] = jnp.dot(
                wt[t * heads:(t + 1) * heads], vbuf[i * per + t], preferred_element_type=F32)
        top_row = jnp.sum(jnp.where(eye, top, 0.0), axis=0, keepdims=True)
        tot_row = jnp.sum(jnp.where(eye, tot, 0.0), axis=0, keepdims=True)
        pad = jnp.zeros((6, n_rows), F32)
        o_ref[i, n_rows:n_rows + 8, :] = jnp.concatenate([top_row, tot_row, pad], axis=0)
        cout(i, 0).start()
        cout(i, 1).start()
        return carry

    lax.fori_loop(0, n_ch, step, 0)
    for i in range(n_ch):
        cout(i, 0).wait()
        cout(i, 1).wait()


def out_kernel(dims, o_ref, h_ref, w_ref, out_ref, rbuf, abuf, attn, lhs, wbuf, pbuf, ybuf, hbuf,
               wsem, hsem, rs_s, rs_r, ab_s, ab_r, y_s, y_r, a_s, a_r, b_s, b_r, d_s, d_r):
    n_tp, n_sp, heads = dims
    nx = n_sp // CORES
    y = lax.axis_index('tp')
    s = lax.axis_index('sp')
    core = lax.rem(s, CORES)
    x = s // CORES
    partner = s + 1 - 2 * core
    _, n_rows, head = attn.shape
    per = n_rows // heads
    depth, cols = wbuf.shape[1:]
    seqs = CORES * per

    def yat(d):
        return lax.rem(y + d, n_tp)

    def xat(d):
        return lax.rem(x + d, nx) * CORES + core

    def wcopy(j):
        return pltpu.make_async_copy(
            w_ref.at[:, ds((core * n_tp + yat(j)) * cols, cols, cols)], wbuf.at[j], wsem.at[j])

    hcopy = pltpu.make_async_copy(
        h_ref.at[ds(x * seqs, seqs, seqs), ds((core * n_tp + y) * cols, cols, cols)], hbuf, hsem)
    order = [d for d in range(1, n_tp)] + [0]
    for j in order:
        wcopy(j).start()
    hcopy.start()

    barrier = pltpu.get_barrier_semaphore()
    for d in range(1, n_sp):
        pl.semaphore_signal(barrier, inc=1, device_id={'sp': lax.rem(s + d, n_sp)}, device_id_type=MESH)
    for d in range(1, n_tp):
        pl.semaphore_signal(barrier, inc=1, device_id={'tp': yat(d)}, device_id_type=MESH)
    pl.semaphore_wait(barrier, n_sp + n_tp - 2)

    def rs(d):
        to = lax.rem(s + d, n_sp)
        return rcopy(o_ref.at[to], rbuf.at[d], rs_s.at[d], rs_r.at[d], sp=to)

    for d in range(1, n_sp):
        rs(d).start()
    parts = [o_ref.at[s]]
    for d in range(1, n_sp):
        rs(d).wait_recv()
        parts.append(rbuf.at[d])
    tops = [p[n_rows:n_rows + 1, :] for p in parts]
    sums = [p[n_rows + 1:n_rows + 2, :] for p in parts]
    top = functools.reduce(jnp.maximum, tops)
    facs = [jnp.exp(t - top) for t in tops]
    tot = functools.reduce(jnp.add, [f * l for f, l in zip(facs, sums)])
    fac = jnp.concatenate([f / tot for f in facs], axis=0)
    pad = jnp.zeros((n_rows - n_sp, n_rows), F32)
    fac = jnp.transpose(jnp.concatenate([fac, pad], axis=0))
    val = parts[0][0:n_rows, :] * fac[:, 0:1]
    for j in range(1, n_sp):
        val = val + parts[j][0:n_rows, :] * fac[:, j:j + 1]
    attn[0] = val

    swap = rcopy(attn.at[0], abuf.at[core], ab_s, ab_r, sp=partner)
    swap.start()
    abuf[core] = val
    swap.wait()
    flat = abuf.reshape(CORES * n_rows, head)
    for n in range(heads):
        lhs[:, n * head:(n + 1) * head] = flat[pl.ds(n, seqs, stride=heads), :].astype(BF16)

    def ysend(d):
        return rcopy(pbuf.at[d], ybuf.at[d], y_s.at[d], y_r.at[d], tp=yat(d))

    def proj(j):
        wcopy(j).wait()
        pbuf[j] = jnp.dot(lhs[...], wbuf[j], preferred_element_type=F32)

    for j in order:
        proj(j)
        if j:
            ysend(j).start()
    hcopy.wait()
    tot = pbuf[0]
    for d in range(1, n_tp):
        ysend(d).wait_recv()
        tot = tot + ybuf[d]
    out_ref[ds(x * seqs, seqs, seqs), ds((core * n_tp + y) * cols, cols, cols)] = hbuf[...].astype(F32) + tot

    def block(dy, dx, part):
        by = lax.rem(y + n_tp - dy, n_tp)
        bx = lax.rem(x + nx - dx, nx)
        return out_ref.at[ds(bx * seqs + part * per, per, per), ds((core * n_tp + by) * cols, cols, cols)]

    sends = []

    def go(dy, dx, part, sems, where, ty, tx):
        ref = block(dy, dx, part)
        cp = rcopy(ref, ref, sems[0].at[ty, tx], sems[1].at[ty, tx], **where)
        cp.start()
        sends.append(cp)

    def fwd(dy, dx, part):
        if part == 0 and dx == 0:
            for e in range(1, nx):
                go(dy, 0, 0, (a_s, a_r), {'sp': xat(e)}, dy, e)
        if part == 1 and dy == 0:
            for e in range(1, n_tp):
                go(0, dx, 1, (b_s, b_r), {'tp': yat(e)}, e, dx)
        ref = block(dy, dx, part)
        cp = rcopy(ref, ref, d_s.at[part, dy, dx], d_r.at[part, dy, dx], sp=partner)
        cp.start()
        sends.append(cp)

    for e in range(1, n_tp):
        go(0, 0, 0, (a_s, a_r), {'tp': yat(e)}, e, 0)
    for e in range(1, nx):
        go(0, 0, 1, (b_s, b_r), {'sp': xat(e)}, 0, e)
    fwd(0, 0, 0)
    fwd(0, 0, 1)

    def arrive(dy, dx, part):
        ref = block(dy, dx, part)
        r = (a_r, b_r)[part].at[dy, dx]
        q = (a_s, b_s)[part].at[dy, dx]
        rcopy(ref, ref, q, r, sp=partner).wait_recv()
        fwd(dy, dx, part)

    for e in range(1, max(n_tp, nx)):
        if e < n_tp:
            arrive(e, 0, 0)
        if e < nx:
            arrive(0, e, 1)
    for dy in range(n_tp):
        for e in range(1, nx):
            arrive(dy, e, 0)
    for dx in range(nx):
        for e in range(1, n_tp):
            arrive(e, dx, 1)
    for part in range(2):
        for dy in range(n_tp):
            for dx in range(nx):
                by = lax.rem(y + n_tp - dy, n_tp)
                bx = lax.rem(x + nx - dx, nx)
                ref = out_ref.at[ds(bx * seqs + part * per, per, per),
                                 ds(((1 - core) * n_tp + by) * cols, cols, cols)]
                rcopy(ref, ref, d_s.at[part, dy, dx], d_r.at[part, dy, dx], sp=partner).wait_recv()
    for cp in sends:
        cp.wait_send()
    for d in range(1, n_sp):
        rs(d).wait_send()
    for d in range(1, n_tp):
        ysend(d).wait_send()


def solution(mesh):
    n_tp, n_sp = mesh.shape['tp'], mesh.shape['sp']
    cache_spec = P('dp', 'sp', 'tp', None)
    DMA = pltpu.SemaphoreType.DMA

    def local_step(hidden, norm_scale, w_qkv, w_out, k_cache, v_cache, positions):
        n_seq, seq_local, kv_local, head = k_cache.shape
        d_model = hidden.shape[1]
        q_per_kv = w_qkv.shape[1] // (kv_local * head) - 2
        heads = kv_local * q_per_kv
        grp_cols = (q_per_kv + 2) * head
        n_blk = 8
        blk = d_model // n_blk
        per = n_seq // n_sp
        n_rows = per * heads

        qkv = pl.pallas_call(
            functools.partial(qkv_kernel, (q_per_kv, head)),
            out_shape=jax.ShapeDtypeStruct((kv_local, n_seq * (q_per_kv + 2), head), F32),
            in_specs=[VMEM, VMEM, VMEM, ANY],
            out_specs=VMEM,
            scratch_shapes=[
                pltpu.VMEM((n_blk, blk, grp_cols), BF16),
                pltpu.VMEM((n_seq, d_model), BF16),
                pltpu.VMEM((n_seq, grp_cols), F32),
                pltpu.VMEM((n_seq * (q_per_kv + 2), head), F32),
                DMA((n_blk,)), DMA, DMA,
            ],
            compiler_params=pltpu.CompilerParams(
                collective_id=0, has_side_effects=True, vmem_limit_bytes=VMEM_LIMIT),
            name='qkv',
        )(hidden, norm_scale.reshape(1, d_model), positions.reshape(1, n_seq), w_qkv)

        flat = (n_seq, seq_local * kv_local, head)
        cache_out = jax.ShapeDtypeStruct(flat, BF16)
        part, k_out, v_out = pl.pallas_call(
            functools.partial(attn_kernel, (q_per_kv, head)),
            out_shape=(jax.ShapeDtypeStruct((n_sp, n_rows + 8, head), F32), cache_out, cache_out),
            in_specs=[SMEM, VMEM, ANY, ANY],
            out_specs=(VMEM, ANY, ANY),
            scratch_shapes=[
                pltpu.VMEM(flat, BF16), pltpu.VMEM(flat, BF16),
                DMA((2, n_sp)), DMA((2, n_sp)),
            ],
            compiler_params=pltpu.CompilerParams(vmem_limit_bytes=VMEM_LIMIT),
            name='attn',
        )(positions, qkv, k_cache.reshape(flat), v_cache.reshape(flat))

        nx = n_sp // CORES
        cols = d_model // (CORES * n_tp)
        depth = w_out.shape[0]
        h_out = pl.pallas_call(
            functools.partial(out_kernel, (n_tp, n_sp, heads)),
            out_shape=jax.ShapeDtypeStruct((n_seq, d_model), F32),
            in_specs=[VMEM, ANY, ANY],
            out_specs=VMEM,
            scratch_shapes=[
                pltpu.VMEM((n_sp, n_rows + 8, head), F32),
                pltpu.VMEM((CORES, n_rows, head), F32),
                pltpu.VMEM((1, n_rows, head), F32),
                pltpu.VMEM((CORES * per, depth), BF16),
                pltpu.VMEM((n_tp, depth, cols), BF16),
                pltpu.VMEM((n_tp, CORES * per, cols), F32),
                pltpu.VMEM((n_tp, CORES * per, cols), F32),
                pltpu.VMEM((CORES * per, cols), BF16),
                DMA((n_tp,)), DMA,
                DMA((n_sp,)), DMA((n_sp,)), DMA, DMA, DMA((n_tp,)), DMA((n_tp,)),
                DMA((n_tp, nx)), DMA((n_tp, nx)), DMA((n_tp, nx)), DMA((n_tp, nx)),
                DMA((2, n_tp, nx)), DMA((2, n_tp, nx)),
            ],
            compiler_params=pltpu.CompilerParams(
                collective_id=1, has_side_effects=True, vmem_limit_bytes=VMEM_LIMIT),
            name='outproj',
        )(part, hidden, w_out)
        return h_out.astype(BF16), k_out.reshape(k_cache.shape), v_out.reshape(v_cache.shape)

    return jax.shard_map(
        local_step,
        mesh=mesh,
        in_specs=(P('dp', None), P(None), P(None, 'tp'), P('tp', None), cache_spec, cache_spec, P('dp')),
        out_specs=(P('dp', None), cache_spec, cache_spec),
        check_vma=False,
    )
```

time: 221 us -> 63.9 us (0.29)
  waiting for transfers between devices: 113 us -> 0 us
  Pallas kernels: 0 us -> 59 us
  matrix products: 37.9 us -> 0 us
  blocking collectives: 24.5 us -> 0 us
  other arithmetic: 24.1 us -> 2.67 us
  between operations: 14.3 us -> 0.65 us
  local copies, waits for them, and re-layouts: 5.68 us -> 1.35 us
    psum x2 -> x0, waiting for transfers between devices: 113 us -> none  [the longest x1 58.6 us: local_step(): merged = lax.psum(packed, 'sp')]
    pallas_call x0 -> x3, Pallas kernels: none -> 59 us  [the longest x1 37 us: local_step(): pl.pallas_call(functools.partial(out_kernel, (n_tp, n_sp, heads)), out_sh...]
    dot_general x4 -> x0, matrix products: 37.9 us -> none  [the longest x1 17.1 us: local_step(): jnp.dot(normed, w_qkv, preferred_element_type=jnp.float32)]
    pmax x1 -> x0, blocking collectives: 24.5 us -> none  [local_step(): global_max = lax.pmax(local_max, 'sp')]
    select_n x1 -> x0, other arithmetic: 13.5 us -> none  [local_step(): v_upd = jnp.where(new_row, grouped[:, :, q_per_kv + 1][:, None], v_cache)]
    reduce_sum x3 -> x0, other arithmetic: 3.56 us -> none  [the longest x1 1.67 us: layer_norm_bf16(): row_var = jnp.mean(centered * centered, axis=-1, keepdims=True)]
    unnamed x8 -> x0, local copies, waits for them, and re-layouts: 3.05 us -> none
    convert_element_type x5 -> x1, other arithmetic: 4.86 us -> 2.67 us  [local_step(): h_out.astype(BF16)]
  transfers between devices with their start and end apart: 2 -> 0, of which waited for: 2 -> 0; matrix products, arithmetic and copies ran while one was open for 0% -> 0% of each run, Pallas kernels for 0% -> 0%
where the time goes in v1:
time: 63.9 us; the launch traced here: 63.6 us
  Pallas kernels  59 us (92%)
  other arithmetic  2.67 us (4%)
  local copies, waits for them, and re-layouts  1.35 us (2%)
  between operations  0.65 us (1%)
    pallas_call x1, Pallas kernels, local_step(): pl.pallas_call(functools.partial(out_kernel, (n_tp, n_sp, heads)), out_sh...  37 us
    pallas_call x1, Pallas kernels, local_step(): pl.pallas_call(functools.partial(qkv_kernel, (q_per_kv, head)), out_shape...  13.1 us
    pallas_call x1, Pallas kernels, local_step(): pl.pallas_call(functools.partial(attn_kernel, (q_per_kv, head)), out_shap...  8.81 us
    convert_element_type x1, other arithmetic, local_step(): h_out.astype(BF16)  2.67 us
    reshape x1, local copies, waits for them, and re-layouts, local_step(): norm_scale.reshape(1, d_model)  1.35 us

profile of v1, /device:TPU:97, one launch (start us, length us, event | category | flops | bytes accessed | tf_op | source)
XLA Modules:
  0.0 63.6 jit_solution(16251165869542787276)
XLA Ops:
  0.6 1.4 %reshape.24.scale_ref = bf16[1,8192]{1,0:T(2,128)(2,1)} reshape(bf16[8192]{0:T(1024)(128)(2,1)} %param.8) | data formatting | bytes 32768 | tf_op jit(solution)/shard_map/reshape | solution.py:363
  2.0 13.1 %qkv.1.qkv_ref = f32[2,640,128]{2,1,0:T(8,128)} custom-call(bf16[64,8192]{1,0:T(8,128)(2,1)} %h_ref.3, bf16[1,8192]{1,0:T(2,128)(2,1)} %reshape.24.scale_ref, s32[1,64]{1,0:T(1,128)} %bitcast.7, bf16[8192,2560]{1,0:T(8,128)(2,1)} %w_ref.2), custom_call_target="tpu_custom_call" | custom-call | tf_op jit(solution)/shard_map/qkv/pallas_call | solution.py:348
  15.1 8.8 %attn.1 = (f32[8,136,128]{2,1,0:T(8,128)}, bf16[64,256,128]{2,1,0:T(8,128)(2,1)}, bf16[64,256,128]{2,1,0:T(8,128)(2,1)}) custom-call(s32[64]{0:T(128)} %pos_ref.1, f32[2,640,128]{2,1,0:T(8,128)} %qkv.1.qkv_ref, bf16[64,256,128]{2,1,0:T(8,128)(2,1)} %bitcast.5, bf16[64,256,128]{2,1,0:T(8,128)(2,1)} %bitcast.6), custom_call_target="tpu_custom_call" | custom-call | tf_op jit(solution)/shard_map/attn/pallas_call | solution.py:367
  23.9 37.0 %outproj.1 = f32[64,8192]{1,0:T(8,128)} custom-call(f32[8,136,128]{2,1,0:T(8,128)} %get-tuple-element.6.o_ref, bf16[64,8192]{1,0:T(8,128)(2,1)} %h_ref.3, bf16[2048,8192]{1,0:T(8,128)(2,1)} %w_ref.3), custom_call_target="tpu_custom_call" | custom-call | tf_op jit(solution)/shard_map/outproj/pallas_call | solution.py:383
  61.0 2.7 %convert_element_type.3 = bf16[64,8192]{1,0:T(8,128)(2,1)} convert(f32[64,8192]{1,0:T(8,128)} %outproj.1) | non-fusion elementwise | flops 524288 | bytes 3145728 | tf_op jit(solution)/shard_map/convert_element_type | solution.py:406

commit v2 on v1

--- a/solution.py
+++ b/solution.py
@@ -11,11 +11,19 @@
 MESH = pl.DeviceIdType.MESH
 F32 = jnp.float32
 BF16 = jnp.bfloat16
-ANY = pl.BlockSpec(memory_space=pl.ANY)
+HBM = pl.BlockSpec(memory_space=pltpu.HBM)
 VMEM = pl.BlockSpec(memory_space=pltpu.VMEM)
 SMEM = pl.BlockSpec(memory_space=pltpu.SMEM)
 CORES = 2
-VMEM_LIMIT = 60 * 1024 * 1024
+MIB = 1024 * 1024
+
+
+def in_vmem(val):
+    return pltpu.with_memory_space_constraint(val, pltpu.VMEM)
+
+
+def in_hbm(val):
+    return pltpu.with_memory_space_constraint(val, pltpu.HBM)
 
 
 def ds(start, size, align):
@@ -29,7 +37,8 @@
     )
 
 
-def qkv_kernel(dims, h_ref, scale_ref, pos_ref, w_ref, out_ref, wbuf, u_ref, acc, mine, wsem, send_sem, recv_sem):
+def qkv_kernel(dims, h_hbm, scale_hbm, pos_hbm, w_ref, out_ref, h_ref, scale_ref, pos_ref, wbuf, u_ref, acc, mine,
+               gain, hsem, wsem, send_sem, recv_sem):
     n_seq, d_model = h_ref.shape
     q_per_kv, head = dims
     n_blk, blk, cols = wbuf.shape
@@ -41,11 +50,20 @@
         return pltpu.make_async_copy(
             w_ref.at[ds(i * blk, blk, blk), ds(core * cols, cols, 128)], wbuf.at[i], wsem.at[i])
 
+    loads = [
+        pltpu.make_async_copy(src, dst, hsem.at[i])
+        for i, (src, dst) in enumerate(((h_hbm, h_ref), (scale_hbm, scale_ref), (pos_hbm, pos_ref)))
+    ]
+    for load in loads:
+        load.start()
     for i in range(n_blk):
         wcopy(i).start()
     barrier = pltpu.get_barrier_semaphore()
     pl.semaphore_signal(barrier, inc=1, device_id={'sp': partner}, device_id_type=MESH)
 
+    for load in loads:
+        load.wait()
+
     lanes = 128
     zero = jnp.zeros((n_seq, lanes), F32)
 
@@ -61,10 +79,12 @@
     var = jnp.sum(lax.fori_loop(0, d_model // lanes, add_sq, zero, unroll=8), axis=1, keepdims=True) / d_model
     inv = lax.rsqrt(var + 1e-5)
 
+    gain[...] = scale_ref[...].astype(F32)
+
     def norm(i, carry):
         cut = ds(i * lanes, lanes, lanes)
         cent = h_ref[:, cut].astype(F32) - mean
-        u_ref[:, cut] = (cent * inv * scale_ref[:, cut].astype(F32)).astype(BF16)
+        u_ref[:, cut] = (cent * inv * gain[pl.ds(i, 1), :]).astype(BF16)
         return carry
 
     lax.fori_loop(0, d_model // lanes, norm, 0, unroll=8)
@@ -102,78 +122,102 @@
     give.wait()
 
 
-def attn_kernel(dims, pos_ref, qkv_ref, k_ref, v_ref, o_ref, ko_ref, vo_ref, kbuf, vbuf, isem, osem):
+def attn_kernel(dims, pos_ref, qkv_ref, k_ref, v_ref, o_ref, ko_ref, vo_ref, kp, vp, osem, psem):
     q_per_kv, head = dims
-    n_seq, rows2, _ = kbuf.shape
-    n_grp = rows2 // qkv_ref.shape[0]
+    n_seq, rows2, _ = k_ref.shape
     groups = qkv_ref.shape[0]
+    n_grp = rows2 // groups
     n_ch = o_ref.shape[0]
     per = n_seq // n_ch
     heads = groups * q_per_kv
     base = lax.axis_index('sp') * n_grp
-
-    def cin(i, which):
-        src, dst = ((k_ref, kbuf), (v_ref, vbuf))[which]
-        return pltpu.make_async_copy(src.at[pl.ds(i * per, per)], dst.at[pl.ds(i * per, per)], isem.at[which, i])
-
-    def cout(i, which):
-        src, dst = ((kbuf, ko_ref), (vbuf, vo_ref))[which]
-        return pltpu.make_async_copy(src.at[pl.ds(i * per, per)], dst.at[pl.ds(i * per, per)], osem.at[which, i])
+    tile = 8 * groups
+    pairs = ((k_ref, ko_ref, kp), (v_ref, vo_ref, vp))
+
+    def bulk(i, which):
+        src, dst, _ = pairs[which]
+        cut = pl.ds(i * per, per)
+        return pltpu.make_async_copy(src.at[cut], dst.at[cut], osem.at[which, i])
 
     for i in range(n_ch):
-        cin(i, 0).start()
-        cin(i, 1).start()
+        bulk(i, 0).start()
+        bulk(i, 1).start()
 
     colj = lax.broadcasted_iota(jnp.int32, (heads, rows2), 1)
     rown = lax.broadcasted_iota(jnp.int32, (heads, rows2), 0)
     same = lax.rem(colj, groups) == rown // q_per_kv
-    tile = 8 * groups
     trow = lax.broadcasted_iota(jnp.int32, (tile, head), 0)
     n_rows = per * heads
     eye = lax.broadcasted_iota(jnp.int32, (n_rows, n_rows), 0) == lax.broadcasted_iota(jnp.int32, (n_rows, n_rows), 1)
     q_rows = n_seq * q_per_kv
 
-    def step(i, carry):
-        cin(i, 0).wait()
-        cin(i, 1).wait()
-        scores = []
+    def locate(b):
+        rel = pos_ref[b] - base
+        at = jnp.clip(rel, 0, n_grp - 1)
+        return rel, at, jnp.logical_and(rel >= 0, rel < n_grp)
+
+    def patch(i):
+        for which in range(2):
+            bulk(i, which).wait()
         for t in range(per):
             b = i * per + t
-            rel = pos_ref[b] - base
-            here = jnp.logical_and(rel >= 0, rel < n_grp)
-            at = jnp.clip(rel, 0, n_grp - 1)
-            start = (at // 8) * tile
+            _, at, _ = locate(b)
+            cut = ds((at // 8) * tile, tile, tile)
+            for which in range(2):
+                _, dst, new = pairs[which]
+                pltpu.make_async_copy(new.at[b], dst.at[b, cut], psem.at[which]).start()
+
+    def step(i, carry):
+        scores, fresh, vals = [], [], []
+        for t in range(per):
+            b = i * per + t
+            rel, at, here = locate(b)
             hit = jnp.logical_and(trow // groups == at % 8, here)
-            for buf, off in ((kbuf, q_rows), (vbuf, q_rows + n_seq)):
-                cut = ds(start, tile, tile)
-                new = qkv_ref[0, pl.ds(off + b, 1), :]
+            cut = ds((at // 8) * tile, tile, tile)
+            rows = []
+            for (src, _, dst), off in zip(pairs, (q_rows, q_rows + n_seq)):
+                mine = [qkv_ref[g, pl.ds(off + b, 1), :] for g in range(groups)]
+                new = mine[0]
                 for g in range(1, groups):
-                    new = jnp.where(trow % groups == g, qkv_ref[g, pl.ds(off + b, 1), :], new)
-                buf[b, cut, :] = jnp.where(hit, new, buf[b, cut, :].astype(F32)).astype(BF16)
+                    new = jnp.where(trow % groups == g, mine[g], new)
+                dst[b] = jnp.where(hit, new, src[b, cut, :].astype(F32)).astype(BF16)
+                rows.append(jnp.concatenate(
+                    [jnp.broadcast_to(m, (q_per_kv, head)) for m in mine], axis=0))
             q = jnp.concatenate([qkv_ref[g, ds(b * q_per_kv, q_per_kv, 8), :] for g in range(groups)], axis=0)
-            sc = lax.dot_general(q.astype(BF16), kbuf[b], (((1,), (1,)), ((), ())), preferred_element_type=F32)
-            ok = jnp.logical_and(same, colj < groups * (rel + 1))
+            sc = lax.dot_general(q.astype(BF16), k_ref[b], (((1,), (1,)), ((), ())), preferred_element_type=F32)
+            ok = jnp.logical_and(same, colj < groups * rel)
             scores.append(jnp.where(ok, sc * (head ** -0.5), -1e30))
+            own = jnp.sum(q * rows[0], axis=1, keepdims=True) * (head ** -0.5)
+            fresh.append(jnp.where(here, own, -1e30))
+            vals.append(rows[1])
         sc = jnp.concatenate(scores, axis=0)
-        top = jnp.max(sc, axis=1, keepdims=True)
+        own = jnp.concatenate(fresh, axis=0)
+        top = jnp.maximum(jnp.max(sc, axis=1, keepdims=True), own)
         wt = jnp.exp(sc - top)
-        tot = jnp.sum(wt, axis=1, keepdims=True)
+        own = jnp.exp(own - top)
+        tot = jnp.sum(wt, axis=1, keepdims=True) + own
         wt = wt.astype(BF16)
+        own = own.astype(BF16).astype(F32)
         for t in range(per):
-            o_ref[i, t * heads:(t + 1) * heads, :] = jnp.dot(
-                wt[t * heads:(t + 1) * heads], vbuf[i * per + t], preferred_element_type=F32)
+            cut = slice(t * heads, (t + 1) * heads)
+            o_ref[i, cut, :] = jnp.dot(
+                wt[cut], v_ref[i * per + t], preferred_element_type=F32) + own[cut] * vals[t]
         top_row = jnp.sum(jnp.where(eye, top, 0.0), axis=0, keepdims=True)
         tot_row = jnp.sum(jnp.where(eye, tot, 0.0), axis=0, keepdims=True)
         pad = jnp.zeros((6, n_rows), F32)
         o_ref[i, n_rows:n_rows + 8, :] = jnp.concatenate([top_row, tot_row, pad], axis=0)
-        cout(i, 0).start()
-        cout(i, 1).start()
+
+        @pl.when(i > 0)
+        def _():
+            patch(i - 1)
+
         return carry
 
     lax.fori_loop(0, n_ch, step, 0)
-    for i in range(n_ch):
-        cout(i, 0).wait()
-        cout(i, 1).wait()
+    patch(n_ch - 1)
+    for which in range(2):
+        _, dst, new = pairs[which]
+        pltpu.make_async_copy(new, dst.at[:, pl.ds(0, tile)], psem.at[which]).wait()
 
 
 def out_kernel(dims, o_ref, h_ref, w_ref, out_ref, rbuf, abuf, attn, lhs, wbuf, pbuf, ybuf, hbuf,
@@ -347,35 +391,41 @@
 
         qkv = pl.pallas_call(
             functools.partial(qkv_kernel, (q_per_kv, head)),
-            out_shape=jax.ShapeDtypeStruct((kv_local, n_seq * (q_per_kv + 2), head), F32),
-            in_specs=[VMEM, VMEM, VMEM, ANY],
+            out_shape=pltpu.VMEM((kv_local, n_seq * (q_per_kv + 2), head), F32),
+            in_specs=[HBM, HBM, HBM, HBM],
             out_specs=VMEM,
             scratch_shapes=[
+                pltpu.VMEM(hidden.shape, BF16),
+                pltpu.VMEM((d_model // 128, 128), BF16),
+                pltpu.VMEM((1, n_seq), jnp.int32),
                 pltpu.VMEM((n_blk, blk, grp_cols), BF16),
                 pltpu.VMEM((n_seq, d_model), BF16),
                 pltpu.VMEM((n_seq, grp_cols), F32),
                 pltpu.VMEM((n_seq * (q_per_kv + 2), head), F32),
-                DMA((n_blk,)), DMA, DMA,
+                pltpu.VMEM((d_model // 128, 128), F32),
+                DMA((3,)), DMA((n_blk,)), DMA, DMA,
             ],
             compiler_params=pltpu.CompilerParams(
-                collective_id=0, has_side_effects=True, vmem_limit_bytes=VMEM_LIMIT),
+                collective_id=0, has_side_effects=True, vmem_limit_bytes=28 * MIB),
             name='qkv',
-        )(hidden, norm_scale.reshape(1, d_model), positions.reshape(1, n_seq), w_qkv)
+        )(in_hbm(hidden), in_hbm(norm_scale.reshape(d_model // 128, 128)),
+          in_hbm(positions.reshape(1, n_seq)), in_hbm(w_qkv))
 
         flat = (n_seq, seq_local * kv_local, head)
         cache_out = jax.ShapeDtypeStruct(flat, BF16)
+        tile = 8 * kv_local
         part, k_out, v_out = pl.pallas_call(
             functools.partial(attn_kernel, (q_per_kv, head)),
-            out_shape=(jax.ShapeDtypeStruct((n_sp, n_rows + 8, head), F32), cache_out, cache_out),
-            in_specs=[SMEM, VMEM, ANY, ANY],
-            out_specs=(VMEM, ANY, ANY),
+            out_shape=(pltpu.VMEM((n_sp, n_rows + 8, head), F32), cache_out, cache_out),
+            in_specs=[SMEM, VMEM, VMEM, VMEM],
+            out_specs=(VMEM, HBM, HBM),
             scratch_shapes=[
-                pltpu.VMEM(flat, BF16), pltpu.VMEM(flat, BF16),
-                DMA((2, n_sp)), DMA((2, n_sp)),
+                pltpu.VMEM((n_seq, tile, head), BF16), pltpu.VMEM((n_seq, tile, head), BF16),
+                DMA((2, n_sp)), DMA((2,)),
             ],
-            compiler_params=pltpu.CompilerParams(vmem_limit_bytes=VMEM_LIMIT),
+            compiler_params=pltpu.CompilerParams(vmem_limit_bytes=4 * MIB),
             name='attn',
-        )(positions, qkv, k_cache.reshape(flat), v_cache.reshape(flat))
+        )(positions, qkv, in_vmem(k_cache.reshape(flat)), in_vmem(v_cache.reshape(flat)))
 
         nx = n_sp // CORES
         cols = d_model // (CORES * n_tp)
@@ -383,7 +433,7 @@
         h_out = pl.pallas_call(
             functools.partial(out_kernel, (n_tp, n_sp, heads)),
             out_shape=jax.ShapeDtypeStruct((n_seq, d_model), F32),
-            in_specs=[VMEM, ANY, ANY],
+            in_specs=[VMEM, HBM, HBM],
             out_specs=VMEM,
             scratch_shapes=[
                 pltpu.VMEM((n_sp, n_rows + 8, head), F32),
@@ -400,9 +450,9 @@
                 DMA((2, n_tp, nx)), DMA((2, n_tp, nx)),
             ],
             compiler_params=pltpu.CompilerParams(
-                collective_id=1, has_side_effects=True, vmem_limit_bytes=VMEM_LIMIT),
+                collective_id=1, has_side_effects=True, vmem_limit_bytes=28 * MIB),
             name='outproj',
-        )(part, hidden, w_out)
+        )(part, in_hbm(hidden), in_hbm(w_out))
         return h_out.astype(BF16), k_out.reshape(k_cache.shape), v_out.reshape(v_cache.shape)
 
     return jax.shard_map(

time: 63.9 us -> 59.8 us (0.936)
  other arithmetic: 2.67 us -> 1.08 us
  local copies, waits for them, and re-layouts: 1.35 us -> 0.01 us
  Pallas kernels: 59 us -> 57.9 us
    pallas_call x1, Pallas kernels: 13.1 us -> 15.9 us  [local_step(): pl.pallas_call(functools.partial(qkv_kernel, (q_per_kv, head)), out_shape...]
    pallas_call x1, Pallas kernels: 8.81 us -> 6.72 us  [local_step(): pl.pallas_call(functools.partial(attn_kernel, (q_per_kv, head)), out_shap...]
    pallas_call x1, Pallas kernels: 37 us -> 35.3 us  [local_step(): pl.pallas_call(functools.partial(out_kernel, (n_tp, n_sp, heads)), out_sh...]
    convert_element_type x1, other arithmetic: 2.67 us -> 1.08 us  [local_step(): h_out.astype(BF16)]
    reshape x1 -> x0, local copies, waits for them, and re-layouts: 1.35 us -> none  [local_step(): norm_scale.reshape(1, d_model)]
where the time goes in v2:
time: 59.8 us; the launch traced here: 59.7 us
  Pallas kernels  57.9 us (97%)
  other arithmetic  1.08 us (2%)
  between operations  0.7 us (1%)
    pallas_call x1, Pallas kernels, local_step(): pl.pallas_call(functools.partial(out_kernel, (n_tp, n_sp, heads)), out_sh...  35.3 us
    pallas_call x1, Pallas kernels, local_step(): pl.pallas_call(functools.partial(qkv_kernel, (q_per_kv, head)), out_shape...  15.9 us
    pallas_call x1, Pallas kernels, local_step(): pl.pallas_call(functools.partial(attn_kernel, (q_per_kv, head)), out_shap...  6.72 us

profile of v2, /device:TPU:97, one launch (start us, length us, event | category | flops | bytes accessed | tf_op | source)
XLA Modules:
  0.0 59.7 jit_solution(472443754492204536)
XLA Ops:
  0.6 0.0 copy-start
  0.6 0.0 copy-start.1
  0.7 0.0 copy-start.2
  0.7 15.9 %qkv.1.qkv_ref = f32[2,640,128]{2,1,0:T(8,128)S(1)} custom-call(bf16[64,8192]{1,0:T(8,128)(2,1)} %h_ref.1, bf16[64,128]{1,0:T(8,128)(2,1)} %bitcast.9, s32[1,64]{1,0:T(1,128)} %bitcast.8, bf16[8192,2560]{1,0:T(8,128)(2,1)} %w_ref.2), custom_call_target="tpu_custom_call" | custom-call | tf_op jit(solution)/shard_map/qkv/pallas_call | solution.py:392
  16.6 0.0 copy-done
  16.6 0.0 copy-done.1
  16.6 0.0 copy-done.2
  16.6 6.7 %attn.1 = (f32[8,136,128]{2,1,0:T(8,128)S(1)}, bf16[64,256,128]{2,1,0:T(8,128)(2,1)}, bf16[64,256,128]{2,1,0:T(8,128)(2,1)}) custom-call(s32[64]{0:T(128)S(1)} %copy-done.2, f32[2,640,128]{2,1,0:T(8,128)S(1)} %qkv.1.qkv_ref, bf16[64,256,128]{2,1,0:T(8,128)(2,1)S(1)} %bitcast.6, bf16[64,256,128]{2,1,0:T(8,128)(2,1)S(1)} %bitcast.7), custom_call_target="tpu_custom_call" | custom-call | tf_op jit(solution)/shard_map/attn/pallas_call | solution.py:417
  23.3 35.3 %outproj.1 = f32[64,8192]{1,0:T(8,128)S(1)} custom-call(f32[8,136,128]{2,1,0:T(8,128)S(1)} %get-tuple-element.6.o_ref, bf16[64,8192]{1,0:T(8,128)(2,1)} %h_ref.1, bf16[2048,8192]{1,0:T(8,128)(2,1)} %w_ref.3), custom_call_target="tpu_custom_call" | custom-call | tf_op jit(solution)/shard_map/outproj/pallas_call | solution.py:433
  58.6 1.1 %convert_element_type.3 = bf16[64,8192]{1,0:T(8,128)(2,1)} convert(f32[64,8192]{1,0:T(8,128)S(1)} %outproj.1) | non-fusion elementwise | flops 524288 | bytes 3145728 | tf_op jit(solution)/shard_map/convert_element_type | solution.py:456
Async XLA Ops:
  0.6 15.9 %copy-start = (bf16[64,128,2,128]{3,2,1,0:T(2,128)(2,1)S(1)}, bf16[64,128,2,128]{3,2,1,0:T(2,128)(2,1)}, u32[]{:S(2)}) copy-start(bf16[64,128,2,128]{3,2,1,0:T(2,128)(2,1)} %param.11) | copy-start | bytes 12582916
  0.6 15.9 %copy-start.1 = (bf16[64,128,2,128]{3,2,1,0:T(2,128)(2,1)S(1)}, bf16[64,128,2,128]{3,2,1,0:T(2,128)(2,1)}, u32[]{:S(2)}) copy-start(bf16[64,128,2,128]{3,2,1,0:T(2,128)(2,1)} %param.12) | copy-start | bytes 12582916
  0.7 15.9 %copy-start.2 = (s32[64]{0:T(128)S(1)}, s32[64]{0:T(128)}, u32[]{:S(2)}) copy-start(s32[64]{0:T(128)} %pos_ref.1) | copy-start | bytes 772

commit v3 on v2

--- a/solution.py
+++ b/solution.py
@@ -15,11 +15,8 @@
 VMEM = pl.BlockSpec(memory_space=pltpu.VMEM)
 SMEM = pl.BlockSpec(memory_space=pltpu.SMEM)
 CORES = 2
+RING_HEADS = 1
 MIB = 1024 * 1024
-
-
-def in_vmem(val):
-    return pltpu.with_memory_space_constraint(val, pltpu.VMEM)
 
 
 def in_hbm(val):
@@ -37,30 +34,46 @@
     )
 
 
-def qkv_kernel(dims, h_hbm, scale_hbm, pos_hbm, w_ref, out_ref, h_ref, scale_ref, pos_ref, wbuf, u_ref, acc, mine,
-               gain, hsem, wsem, send_sem, recv_sem):
+def qkv_kernel(dims, h_hbm, scale_hbm, pos_hbm, w_ref, k_hbm, v_hbm, out_ref, kbuf, vbuf, h_ref, scale_ref, pos_ref,
+               wring, wloc, u_ref, acc, gain, hsem, rsem, wsem, csem, s_ring, r_ring, s_part, r_part):
     n_seq, d_model = h_ref.shape
-    q_per_kv, head = dims
-    n_blk, blk, cols = wbuf.shape
+    q_per_kv, head, n_sp = dims
+    nx = n_sp // CORES
+    n_rblk, rblk, rcols = wring.shape
+    n_blk, blk, lcols = wloc.shape
+    rh = rcols // head
+    grp = (q_per_kv + 2) * head
     s = lax.axis_index('sp')
     core = lax.rem(s, CORES)
+    x = s // CORES
     partner = s + 1 - 2 * core
 
-    def wcopy(i):
+    def rload(i):
         return pltpu.make_async_copy(
-            w_ref.at[ds(i * blk, blk, blk), ds(core * cols, cols, 128)], wbuf.at[i], wsem.at[i])
+            w_ref.at[ds(i * rblk, rblk, rblk), ds(core * grp + x * rcols, rcols, 128)], wring.at[i], rsem.at[i])
+
+    def wload(i):
+        return pltpu.make_async_copy(
+            w_ref.at[ds(i * blk, blk, blk), ds(core * grp + nx * rcols, lcols, 128)], wloc.at[i], wsem.at[i])
 
     loads = [
         pltpu.make_async_copy(src, dst, hsem.at[i])
         for i, (src, dst) in enumerate(((h_hbm, h_ref), (scale_hbm, scale_ref), (pos_hbm, pos_ref)))
     ]
+    caches = [
+        pltpu.make_async_copy(src, dst, csem.at[i]) for i, (src, dst) in enumerate(((k_hbm, kbuf), (v_hbm, vbuf)))
+    ]
     for load in loads:
         load.start()
+    for i in range(n_rblk):
+        rload(i).start()
     for i in range(n_blk):
-        wcopy(i).start()
+        wload(i).start()
     barrier = pltpu.get_barrier_semaphore()
     pl.semaphore_signal(barrier, inc=1, device_id={'sp': partner}, device_id_type=MESH)
-
+    for d in range(1, nx):
+        pl.semaphore_signal(
+            barrier, inc=1, device_id={'sp': lax.rem(x + d, nx) * CORES + core}, device_id_type=MESH)
     for load in loads:
         load.wait()
 
@@ -98,28 +111,58 @@
     cos_t = jnp.cos(angle)
     sin_t = jnp.where(lane < half, -jnp.sin(angle), jnp.sin(angle))
 
+    def finish(val, rotate):
+        val = jnp.clip(val.astype(BF16), -8.0, 8.0).astype(F32)
+        if rotate:
+            val = (val * cos_t + pltpu.roll(val, half, 1) * sin_t).astype(BF16).astype(F32)
+        return val
+
+    def slab(cx):
+        return out_ref.at[core, ds(cx * rh * n_seq, rh * n_seq, 8)]
+
+    def rsend(d):
+        return rcopy(slab(x), slab(x), s_ring.at[d], r_ring.at[d], sp=lax.rem(x + d, nx) * CORES + core)
+
+    def psend(d):
+        ref = slab(lax.rem(x + nx - d, nx)) if d < nx else out_ref.at[core, pl.ds(nx * rh * n_seq, lcols // head * n_seq)]
+        return rcopy(ref, ref, s_part.at[d], r_part.at[d], sp=partner)
+
+    tot = None
+    for i in range(n_rblk):
+        rload(i).wait()
+        prod = jnp.dot(u_ref[:, i * rblk:(i + 1) * rblk], wring[i], preferred_element_type=F32)
+        tot = prod if tot is None else tot + prod
+    for j in range(rh):
+        out_ref[core, ds((x * rh + j) * n_seq, n_seq, n_seq), :] = finish(tot[:, j * head:(j + 1) * head], True)
+    pl.semaphore_wait(barrier, nx)
+    order = [2, 1, 3] if nx == 4 else list(range(1, nx))
+    for d in order:
+        rsend(d).start()
+    psend(0).start()
+    for cp in caches:
+        cp.start()
+
     acc[...] = jnp.zeros_like(acc)
 
     def mm(i, carry):
-        wcopy(i).wait()
-        acc[...] += jnp.dot(u_ref[:, ds(i * blk, blk, blk)], wbuf[i], preferred_element_type=F32)
+        wload(i).wait()
+        acc[...] += jnp.dot(u_ref[:, ds(i * blk, blk, blk)], wloc[i], preferred_element_type=F32)
         return carry
 
     lax.fori_loop(0, n_blk, mm, 0)
-
-    for j in range(q_per_kv + 2):
-        val = jnp.clip(acc[:, j * head:(j + 1) * head].astype(BF16), -8.0, 8.0).astype(F32)
-        if j < q_per_kv + 1:
-            val = (val * cos_t + pltpu.roll(val, half, 1) * sin_t).astype(BF16).astype(F32)
-        if j < q_per_kv:
-            mine[pl.ds(j, n_seq, stride=q_per_kv), :] = val
-        else:
-            mine[pl.ds((j * n_seq), n_seq), :] = val
-    pl.semaphore_wait(barrier, 1)
-    give = rcopy(mine, out_ref.at[core], send_sem, recv_sem, sp=partner)
-    give.start()
-    out_ref[core] = mine[...]
-    give.wait()
+    for j in range(lcols // head):
+        at = nx * rh + j
+        out_ref[core, at * n_seq:(at + 1) * n_seq, :] = finish(acc[:, j * head:(j + 1) * head], at < q_per_kv + 1)
+    psend(nx).start()
+    for d in list(reversed(order)):
+        rsend(d).wait_recv()
+        psend(d).start()
+    for d in range(nx + 1):
+        psend(d).wait()
+    for d in order:
+        rsend(d).wait_send()
+    for cp in caches:
+        cp.wait()
 
 
 def attn_kernel(dims, pos_ref, qkv_ref, k_ref, v_ref, o_ref, ko_ref, vo_ref, kp, vp, osem, psem):
@@ -156,34 +199,55 @@
         at = jnp.clip(rel, 0, n_grp - 1)
         return rel, at, jnp.logical_and(rel >= 0, rel < n_grp)
 
-    def patch(i):
-        for which in range(2):
-            bulk(i, which).wait()
-        for t in range(per):
-            b = i * per + t
-            _, at, _ = locate(b)
-            cut = ds((at // 8) * tile, tile, tile)
-            for which in range(2):
-                _, dst, new = pairs[which]
-                pltpu.make_async_copy(new.at[b], dst.at[b, cut], psem.at[which]).start()
+    def fresh_row(off, b):
+        return [qkv_ref[g, pl.ds(off + b, 1), :] for g in range(groups)]
+
+    def patch(b, which):
+        _, at, _ = locate(b)
+        _, dst, new = pairs[which]
+        return pltpu.make_async_copy(new.at[b], dst.at[b, ds((at // 8) * tile, tile, tile)], psem.at[which])
+
+    def build(b, carry):
+        _, at, here = locate(b)
+
+        @pl.when(here)
+        def _():
+            for (src, _, dst), off in zip(pairs, (q_rows, q_rows + n_seq)):
+                mine = fresh_row(off, b)
+                new = mine[0]
+                for g in range(1, groups):
+                    new = jnp.where(trow % groups == g, mine[g], new)
+                old = src[b, ds((at // 8) * tile, tile, tile), :].astype(F32)
+                dst[b] = jnp.where(trow // groups == at % 8, new, old).astype(BF16)
+
+        return carry
+
+    def send(b, carry):
+        @pl.when(locate(b)[2])
+        def _():
+            patch(b, 0).start()
+            patch(b, 1).start()
+
+        return carry
+
+    def drain(b, carry):
+        @pl.when(locate(b)[2])
+        def _():
+            patch(b, 0).wait()
+            patch(b, 1).wait()
+
+        return carry
 
     def step(i, carry):
         scores, fresh, vals = [], [], []
         for t in range(per):
             b = i * per + t
             rel, at, here = locate(b)
-            hit = jnp.logical_and(trow // groups == at % 8, here)
-            cut = ds((at // 8) * tile, tile, tile)
-            rows = []
-            for (src, _, dst), off in zip(pairs, (q_rows, q_rows + n_seq)):
-                mine = [qkv_ref[g, pl.ds(off + b, 1), :] for g in range(groups)]
-                new = mine[0]
-                for g in range(1, groups):
-                    new = jnp.where(trow % groups == g, mine[g], new)
-                dst[b] = jnp.where(hit, new, src[b, cut, :].astype(F32)).astype(BF16)
-                rows.append(jnp.concatenate(
-                    [jnp.broadcast_to(m, (q_per_kv, head)) for m in mine], axis=0))
-            q = jnp.concatenate([qkv_ref[g, ds(b * q_per_kv, q_per_kv, 8), :] for g in range(groups)], axis=0)
+            rows = [
+                jnp.concatenate([jnp.broadcast_to(m, (q_per_kv, head)) for m in fresh_row(off, b)], axis=0)
+                for off in (q_rows, q_rows + n_seq)
+            ]
+            q = jnp.concatenate([qkv_ref[g, pl.ds(b, q_per_kv, stride=n_seq), :] for g in range(groups)], axis=0)
             sc = lax.dot_general(q.astype(BF16), k_ref[b], (((1,), (1,)), ((), ())), preferred_element_type=F32)
             ok = jnp.logical_and(same, colj < groups * rel)
             scores.append(jnp.where(ok, sc * (head ** -0.5), -1e30))
@@ -206,18 +270,15 @@
         tot_row = jnp.sum(jnp.where(eye, tot, 0.0), axis=0, keepdims=True)
         pad = jnp.zeros((6, n_rows), F32)
         o_ref[i, n_rows:n_rows + 8, :] = jnp.concatenate([top_row, tot_row, pad], axis=0)
-
-        @pl.when(i > 0)
-        def _():
-            patch(i - 1)
-
         return carry
 
+    lax.fori_loop(0, n_seq, build, 0)
     lax.fori_loop(0, n_ch, step, 0)
-    patch(n_ch - 1)
-    for which in range(2):
-        _, dst, new = pairs[which]
-        pltpu.make_async_copy(new, dst.at[:, pl.ds(0, tile)], psem.at[which]).wait()
+    for i in range(n_ch):
+        bulk(i, 0).wait()
+        bulk(i, 1).wait()
+    lax.fori_loop(0, n_seq, send, 0)
+    lax.fori_loop(0, n_seq, drain, 0)
 
 
 def out_kernel(dims, o_ref, h_ref, w_ref, out_ref, rbuf, abuf, attn, lhs, wbuf, pbuf, ybuf, hbuf,
@@ -384,34 +445,39 @@
         q_per_kv = w_qkv.shape[1] // (kv_local * head) - 2
         heads = kv_local * q_per_kv
         grp_cols = (q_per_kv + 2) * head
-        n_blk = 8
-        blk = d_model // n_blk
+        n_blk, n_rblk = 8, 2
+        nx = n_sp // CORES
+        ring_cols = RING_HEADS * head
+        local_cols = grp_cols - nx * ring_cols
         per = n_seq // n_sp
         n_rows = per * heads
-
-        qkv = pl.pallas_call(
-            functools.partial(qkv_kernel, (q_per_kv, head)),
-            out_shape=pltpu.VMEM((kv_local, n_seq * (q_per_kv + 2), head), F32),
-            in_specs=[HBM, HBM, HBM, HBM],
-            out_specs=VMEM,
+        flat = (n_seq, seq_local * kv_local, head)
+
+        qkv, k_now, v_now = pl.pallas_call(
+            functools.partial(qkv_kernel, (q_per_kv, head, n_sp)),
+            out_shape=(pltpu.VMEM((kv_local, n_seq * (q_per_kv + 2), head), F32),
+                       pltpu.VMEM(flat, BF16), pltpu.VMEM(flat, BF16)),
+            in_specs=[HBM] * 6,
+            out_specs=(VMEM, VMEM, VMEM),
             scratch_shapes=[
                 pltpu.VMEM(hidden.shape, BF16),
                 pltpu.VMEM((d_model // 128, 128), BF16),
                 pltpu.VMEM((1, n_seq), jnp.int32),
-                pltpu.VMEM((n_blk, blk, grp_cols), BF16),
+                pltpu.VMEM((n_rblk, d_model // n_rblk, ring_cols), BF16),
+                pltpu.VMEM((n_blk, d_model // n_blk, local_cols), BF16),
                 pltpu.VMEM((n_seq, d_model), BF16),
-                pltpu.VMEM((n_seq, grp_cols), F32),
-                pltpu.VMEM((n_seq * (q_per_kv + 2), head), F32),
+                pltpu.VMEM((n_seq, local_cols), F32),
                 pltpu.VMEM((d_model // 128, 128), F32),
-                DMA((3,)), DMA((n_blk,)), DMA, DMA,
+                DMA((3,)), DMA((n_rblk,)), DMA((n_blk,)), DMA((2,)),
+                DMA((nx,)), DMA((nx,)), DMA((nx + 1,)), DMA((nx + 1,)),
             ],
             compiler_params=pltpu.CompilerParams(
-                collective_id=0, has_side_effects=True, vmem_limit_bytes=28 * MIB),
+                collective_id=0, has_side_effects=True, vmem_limit_bytes=24 * MIB),
             name='qkv',
         )(in_hbm(hidden), in_hbm(norm_scale.reshape(d_model // 128, 128)),
-          in_hbm(positions.reshape(1, n_seq)), in_hbm(w_qkv))
-
-        flat = (n_seq, seq_local * kv_local, head)
+          in_hbm(positions.reshape(1, n_seq)), in_hbm(w_qkv), in_hbm(k_cache.reshape(flat)),
+          in_hbm(v_cache.reshape(flat)))
+
         cache_out = jax.ShapeDtypeStruct(flat, BF16)
         tile = 8 * kv_local
         part, k_out, v_out = pl.pallas_call(
@@ -425,9 +491,8 @@
             ],
             compiler_params=pltpu.CompilerParams(vmem_limit_bytes=4 * MIB),
             name='attn',
-        )(positions, qkv, in_vmem(k_cache.reshape(flat)), in_vmem(v_cache.reshape(flat)))
-
-        nx = n_sp // CORES
+        )(positions, qkv, k_now, v_now)
+
         cols = d_model // (CORES * n_tp)
         depth = w_out.shape[0]
         h_out = pl.pallas_call(

time: 59.8 us -> 61.4 us (1.027)
  Pallas kernels: 57.9 us -> 59.6 us
    pallas_call x1, Pallas kernels: 6.72 us -> 8.96 us  [local_step(): pl.pallas_call(functools.partial(attn_kernel, (q_per_kv, head)), out_shap...]
    pallas_call x1, Pallas kernels: 15.9 us -> 15.3 us  [local_step(): pl.pallas_call(functools.partial(qkv_kernel, (q_per_kv, head, n_sp)), out...]
where the time goes in v3:
time: 61.4 us; the launch traced here: 61.3 us
  Pallas kernels  59.6 us (97%)
  other arithmetic  1.08 us (2%)
  between operations  0.67 us (1%)
    pallas_call x1, Pallas kernels, local_step(): pl.pallas_call(functools.partial(out_kernel, (n_tp, n_sp, heads)), out_sh...  35.4 us
    pallas_call x1, Pallas kernels, local_step(): pl.pallas_call(functools.partial(qkv_kernel, (q_per_kv, head, n_sp)), out...  15.3 us
    pallas_call x1, Pallas kernels, local_step(): pl.pallas_call(functools.partial(attn_kernel, (q_per_kv, head)), out_shap...  8.96 us

profile of v3, /device:TPU:97, one launch (start us, length us, event | category | flops | bytes accessed | tf_op | source)
XLA Modules:
  0.0 61.3 jit_solution(9702249518226682931)
XLA Ops:
  0.6 0.0 copy-start
  0.6 15.3 %qkv.1 = (f32[2,640,128]{2,1,0:T(8,128)S(1)}, bf16[64,256,128]{2,1,0:T(8,128)(2,1)S(1)}, bf16[64,256,128]{2,1,0:T(8,128)(2,1)S(1)}) custom-call(bf16[64,8192]{1,0:T(8,128)(2,1)} %h_ref.1, bf16[64,128]{1,0:T(8,128)(2,1)} %bitcast.9, s32[1,64]{1,0:T(1,128)} %bitcast.6, bf16[8192,2560]{1,0:T(8,128)(2,1)} %w_ref.2, bf16[64,256,128]{2,1,0:T(8,128)(2,1)} %bitcast.7, ...), custom_call_target="tpu_custom_call" | custom-call | tf_op jit(solution)/shard_map/qkv/pallas_call | solution.py:456
  15.9 0.0 copy-done
  15.9 9.0 %attn.1 = (f32[8,136,128]{2,1,0:T(8,128)S(1)}, bf16[64,256,128]{2,1,0:T(8,128)(2,1)}, bf16[64,256,128]{2,1,0:T(8,128)(2,1)}) custom-call(s32[64]{0:T(128)S(1)} %copy-done, f32[2,640,128]{2,1,0:T(8,128)S(1)} %get-tuple-element.9.qkv_ref, bf16[64,256,128]{2,1,0:T(8,128)(2,1)S(1)} %get-tuple-element.10.k_ref, bf16[64,256,128]{2,1,0:T(8,128)(2,1)S(1)} %get-tuple-element.11.v_ref), custom_call_target="tpu_custom_call" | custom-call | tf_op jit(solution)/shard_map/attn/pallas_call | solution.py:483
  24.9 35.4 %outproj.1 = f32[64,8192]{1,0:T(8,128)S(1)} custom-call(f32[8,136,128]{2,1,0:T(8,128)S(1)} %get-tuple-element.12.o_ref, bf16[64,8192]{1,0:T(8,128)(2,1)} %h_ref.1, bf16[2048,8192]{1,0:T(8,128)(2,1)} %w_ref.3), custom_call_target="tpu_custom_call" | custom-call | tf_op jit(solution)/shard_map/outproj/pallas_call | solution.py:498
  60.3 1.1 %convert_element_type.3 = bf16[64,8192]{1,0:T(8,128)(2,1)} convert(f32[64,8192]{1,0:T(8,128)S(1)} %outproj.1) | non-fusion elementwise | flops 524288 | bytes 3145728 | tf_op jit(solution)/shard_map/convert_element_type | solution.py:521
Async XLA Ops:
  0.6 15.3 %copy-start = (s32[64]{0:T(128)S(1)}, s32[64]{0:T(128)}, u32[]{:S(2)}) copy-start(s32[64]{0:T(128)} %pos_ref.1) | copy-start | bytes 772

commit v4 on v1

--- a/solution.py
+++ b/solution.py
@@ -11,11 +11,15 @@
 MESH = pl.DeviceIdType.MESH
 F32 = jnp.float32
 BF16 = jnp.bfloat16
-ANY = pl.BlockSpec(memory_space=pl.ANY)
+HBM = pl.BlockSpec(memory_space=pltpu.HBM)
 VMEM = pl.BlockSpec(memory_space=pltpu.VMEM)
 SMEM = pl.BlockSpec(memory_space=pltpu.SMEM)
 CORES = 2
-VMEM_LIMIT = 60 * 1024 * 1024
+MIB = 1024 * 1024
+
+
+def in_hbm(val):
+    return pltpu.with_memory_space_constraint(val, pltpu.HBM)
 
 
 def ds(start, size, align):
@@ -29,22 +33,36 @@
     )
 
 
-def qkv_kernel(dims, h_ref, scale_ref, pos_ref, w_ref, out_ref, wbuf, u_ref, acc, mine, wsem, send_sem, recv_sem):
+def qkv_kernel(dims, h_hbm, scale_hbm, pos_hbm, w_ref, k_hbm, v_hbm, out_ref, kbuf, vbuf, h_ref, scale_ref, pos_ref,
+               wbuf, u_ref, gain, hsem, wsem, csem, s_part, r_part):
     n_seq, d_model = h_ref.shape
-    q_per_kv, head = dims
-    n_blk, blk, cols = wbuf.shape
+    q_per_kv, head, pitch = dims
+    n_blk, n_half, blk, cols = wbuf.shape
+    grp = (q_per_kv + 2) * head
     s = lax.axis_index('sp')
     core = lax.rem(s, CORES)
     partner = s + 1 - 2 * core
 
-    def wcopy(i):
+    def wload(i, k):
         return pltpu.make_async_copy(
-            w_ref.at[ds(i * blk, blk, blk), ds(core * cols, cols, 128)], wbuf.at[i], wsem.at[i])
-
+            w_ref.at[pl.ds(k * blk, blk), ds(core * grp + i * cols, cols, 128)], wbuf.at[i, k], wsem.at[i, k])
+
+    loads = [
+        pltpu.make_async_copy(src, dst, hsem.at[i])
+        for i, (src, dst) in enumerate(((h_hbm, h_ref), (scale_hbm, scale_ref), (pos_hbm, pos_ref)))
+    ]
+    caches = [
+        pltpu.make_async_copy(src, dst, csem.at[i]) for i, (src, dst) in enumerate(((k_hbm, kbuf), (v_hbm, vbuf)))
+    ]
+    for load in loads:
+        load.start()
     for i in range(n_blk):
-        wcopy(i).start()
+        for k in range(n_half):
+            wload(i, k).start()
     barrier = pltpu.get_barrier_semaphore()
     pl.semaphore_signal(barrier, inc=1, device_id={'sp': partner}, device_id_type=MESH)
+    for load in loads:
+        load.wait()
 
     lanes = 128
     zero = jnp.zeros((n_seq, lanes), F32)
@@ -61,10 +79,12 @@
     var = jnp.sum(lax.fori_loop(0, d_model // lanes, add_sq, zero, unroll=8), axis=1, keepdims=True) / d_model
     inv = lax.rsqrt(var + 1e-5)
 
+    gain[...] = scale_ref[...].astype(F32)
+
     def norm(i, carry):
         cut = ds(i * lanes, lanes, lanes)
         cent = h_ref[:, cut].astype(F32) - mean
-        u_ref[:, cut] = (cent * inv * scale_ref[:, cut].astype(F32)).astype(BF16)
+        u_ref[:, cut] = (cent * inv * gain[pl.ds(i, 1), :]).astype(BF16)
         return carry
 
     lax.fori_loop(0, d_model // lanes, norm, 0, unroll=8)
@@ -78,51 +98,51 @@
     cos_t = jnp.cos(angle)
     sin_t = jnp.where(lane < half, -jnp.sin(angle), jnp.sin(angle))
 
-    acc[...] = jnp.zeros_like(acc)
-
-    def mm(i, carry):
-        wcopy(i).wait()
-        acc[...] += jnp.dot(u_ref[:, ds(i * blk, blk, blk)], wbuf[i], preferred_element_type=F32)
-        return carry
-
-    lax.fori_loop(0, n_blk, mm, 0)
-
+    def psend(j):
+        ref = out_ref.at[core, pl.ds(j * pitch, n_seq)]
+        return rcopy(ref, ref, s_part.at[j], r_part.at[j], sp=partner)
+
+    for i in range(n_blk):
+        tot = None
+        for k in range(n_half):
+            wload(i, k).wait()
+            prod = jnp.dot(u_ref[:, k * blk:(k + 1) * blk], wbuf[i, k], preferred_element_type=F32)
+            tot = prod if tot is None else tot + prod
+        per_blk = cols // head
+        for t in range(per_blk):
+            j = i * per_blk + t
+            val = jnp.clip(tot[:, t * head:(t + 1) * head].astype(BF16), -8.0, 8.0).astype(F32)
+            if j < q_per_kv + 1:
+                val = (val * cos_t + pltpu.roll(val, half, 1) * sin_t).astype(BF16).astype(F32)
+            out_ref[core, j * pitch:j * pitch + n_seq, :] = val
+        if i == 0:
+            pl.semaphore_wait(barrier, 1)
+        for t in range(per_blk):
+            psend(i * per_blk + t).start()
+        if i == 1:
+            caches[0].start()
+        if i == 2:
+            caches[1].start()
     for j in range(q_per_kv + 2):
-        val = jnp.clip(acc[:, j * head:(j + 1) * head].astype(BF16), -8.0, 8.0).astype(F32)
-        if j < q_per_kv + 1:
-            val = (val * cos_t + pltpu.roll(val, half, 1) * sin_t).astype(BF16).astype(F32)
-        if j < q_per_kv:
-            mine[pl.ds(j, n_seq, stride=q_per_kv), :] = val
-        else:
-            mine[pl.ds((j * n_seq), n_seq), :] = val
-    pl.semaphore_wait(barrier, 1)
-    give = rcopy(mine, out_ref.at[core], send_sem, recv_sem, sp=partner)
-    give.start()
-    out_ref[core] = mine[...]
-    give.wait()
-
-
-def attn_kernel(dims, pos_ref, qkv_ref, k_ref, v_ref, o_ref, ko_ref, vo_ref, kbuf, vbuf, isem, osem):
-    q_per_kv, head = dims
+        psend(j).wait()
+    for cp in caches:
+        cp.wait()
+
+
+def attn_kernel(dims, pos_ref, qkv_ref, k_ref, v_ref, o_ref, ko_ref, vo_ref, kbuf, vbuf, osem):
+    q_per_kv, head, pitch = dims
     n_seq, rows2, _ = kbuf.shape
-    n_grp = rows2 // qkv_ref.shape[0]
     groups = qkv_ref.shape[0]
+    n_grp = rows2 // groups
     n_ch = o_ref.shape[0]
     per = n_seq // n_ch
     heads = groups * q_per_kv
     base = lax.axis_index('sp') * n_grp
 
-    def cin(i, which):
-        src, dst = ((k_ref, kbuf), (v_ref, vbuf))[which]
-        return pltpu.make_async_copy(src.at[pl.ds(i * per, per)], dst.at[pl.ds(i * per, per)], isem.at[which, i])
-
-    def cout(i, which):
+    def bulk(i, which):
         src, dst = ((kbuf, ko_ref), (vbuf, vo_ref))[which]
-        return pltpu.make_async_copy(src.at[pl.ds(i * per, per)], dst.at[pl.ds(i * per, per)], osem.at[which, i])
-
-    for i in range(n_ch):
-        cin(i, 0).start()
-        cin(i, 1).start()
+        cut = pl.ds(i * per, per)
+        return pltpu.make_async_copy(src.at[cut], dst.at[cut], osem.at[which, i])
 
     colj = lax.broadcasted_iota(jnp.int32, (heads, rows2), 1)
     rown = lax.broadcasted_iota(jnp.int32, (heads, rows2), 0)
@@ -131,26 +151,27 @@
     trow = lax.broadcasted_iota(jnp.int32, (tile, head), 0)
     n_rows = per * heads
     eye = lax.broadcasted_iota(jnp.int32, (n_rows, n_rows), 0) == lax.broadcasted_iota(jnp.int32, (n_rows, n_rows), 1)
-    q_rows = n_seq * q_per_kv
 
     def step(i, carry):
-        cin(i, 0).wait()
-        cin(i, 1).wait()
+        @pl.when(i > 0)
+        def _():
+            bulk(i - 1, 0).start()
+            bulk(i - 1, 1).start()
+
         scores = []
         for t in range(per):
             b = i * per + t
             rel = pos_ref[b] - base
             here = jnp.logical_and(rel >= 0, rel < n_grp)
             at = jnp.clip(rel, 0, n_grp - 1)
-            start = (at // 8) * tile
+            cut = ds((at // 8) * tile, tile, tile)
             hit = jnp.logical_and(trow // groups == at % 8, here)
-            for buf, off in ((kbuf, q_rows), (vbuf, q_rows + n_seq)):
-                cut = ds(start, tile, tile)
+            for src, buf, off in ((k_ref, kbuf, q_per_kv * pitch), (v_ref, vbuf, (q_per_kv + 1) * pitch)):
                 new = qkv_ref[0, pl.ds(off + b, 1), :]
                 for g in range(1, groups):
                     new = jnp.where(trow % groups == g, qkv_ref[g, pl.ds(off + b, 1), :], new)
-                buf[b, cut, :] = jnp.where(hit, new, buf[b, cut, :].astype(F32)).astype(BF16)
-            q = jnp.concatenate([qkv_ref[g, ds(b * q_per_kv, q_per_kv, 8), :] for g in range(groups)], axis=0)
+                buf[b, cut, :] = jnp.where(hit, new, src[b, cut, :].astype(F32)).astype(BF16)
+            q = jnp.concatenate([qkv_ref[g, pl.ds(b, q_per_kv, stride=pitch), :] for g in range(groups)], axis=0)
             sc = lax.dot_general(q.astype(BF16), kbuf[b], (((1,), (1,)), ((), ())), preferred_element_type=F32)
             ok = jnp.logical_and(same, colj < groups * (rel + 1))
             scores.append(jnp.where(ok, sc * (head ** -0.5), -1e30))
@@ -166,14 +187,14 @@
         tot_row = jnp.sum(jnp.where(eye, tot, 0.0), axis=0, keepdims=True)
         pad = jnp.zeros((6, n_rows), F32)
         o_ref[i, n_rows:n_rows + 8, :] = jnp.concatenate([top_row, tot_row, pad], axis=0)
-        cout(i, 0).start()
-        cout(i, 1).start()
         return carry
 
     lax.fori_loop(0, n_ch, step, 0)
+    bulk(n_ch - 1, 0).start()
+    bulk(n_ch - 1, 1).start()
     for i in range(n_ch):
-        cout(i, 0).wait()
-        cout(i, 1).wait()
+        bulk(i, 0).wait()
+        bulk(i, 1).wait()
 
 
 def out_kernel(dims, o_ref, h_ref, w_ref, out_ref, rbuf, abuf, attn, lhs, wbuf, pbuf, ybuf, hbuf,
@@ -340,42 +361,46 @@
         q_per_kv = w_qkv.shape[1] // (kv_local * head) - 2
         heads = kv_local * q_per_kv
         grp_cols = (q_per_kv + 2) * head
-        n_blk = 8
-        blk = d_model // n_blk
+        n_blk, n_half = (q_per_kv + 2) // 2, 2
+        pitch = n_seq + 8
         per = n_seq // n_sp
         n_rows = per * heads
-
-        qkv = pl.pallas_call(
-            functools.partial(qkv_kernel, (q_per_kv, head)),
-            out_shape=jax.ShapeDtypeStruct((kv_local, n_seq * (q_per_kv + 2), head), F32),
-            in_specs=[VMEM, VMEM, VMEM, ANY],
-            out_specs=VMEM,
+        flat = (n_seq, seq_local * kv_local, head)
+        vmem_cache = pltpu.VMEM(flat, BF16)
+        hbm_cache = jax.ShapeDtypeStruct(flat, BF16)
+
+        qkv, k_now, v_now = pl.pallas_call(
+            functools.partial(qkv_kernel, (q_per_kv, head, pitch)),
+            out_shape=(pltpu.VMEM((kv_local, pitch * (q_per_kv + 2), head), F32), vmem_cache, vmem_cache),
+            in_specs=[HBM] * 6,
+            out_specs=(VMEM, VMEM, VMEM),
             scratch_shapes=[
-                pltpu.VMEM((n_blk, blk, grp_cols), BF16),
+                pltpu.VMEM(hidden.shape, BF16),
+                pltpu.VMEM((d_model // 128, 128), BF16),
+                pltpu.VMEM((1, n_seq), jnp.int32),
+                pltpu.VMEM((n_blk, n_half, d_model // n_half, grp_cols // n_blk), BF16),
                 pltpu.VMEM((n_seq, d_model), BF16),
-                pltpu.VMEM((n_seq, grp_cols), F32),
-                pltpu.VMEM((n_seq * (q_per_kv + 2), head), F32),
-                DMA((n_blk,)), DMA, DMA,
+                pltpu.VMEM((d_model // 128, 128), F32),
+                DMA((3,)), DMA((n_blk, n_half)), DMA((2,)),
+                DMA((q_per_kv + 2,)), DMA((q_per_kv + 2,)),
             ],
             compiler_params=pltpu.CompilerParams(
-                collective_id=0, has_side_effects=True, vmem_limit_bytes=VMEM_LIMIT),
+                collective_id=0, has_side_effects=True, vmem_limit_bytes=28 * MIB),
             name='qkv',
-        )(hidden, norm_scale.reshape(1, d_model), positions.reshape(1, n_seq), w_qkv)
-
-        flat = (n_seq, seq_local * kv_local, head)
-        cache_out = jax.ShapeDtypeStruct(flat, BF16)
-        part, k_out, v_out = pl.pallas_call(
-            functools.partial(attn_kernel, (q_per_kv, head)),
-            out_shape=(jax.ShapeDtypeStruct((n_sp, n_rows + 8, head), F32), cache_out, cache_out),
-            in_specs=[SMEM, VMEM, ANY, ANY],
-            out_specs=(VMEM, ANY, ANY),
-            scratch_shapes=[
-                pltpu.VMEM(flat, BF16), pltpu.VMEM(flat, BF16),
-                DMA((2, n_sp)), DMA((2, n_sp)),
-            ],
-            compiler_params=pltpu.CompilerParams(vmem_limit_bytes=VMEM_LIMIT),
+        )(in_hbm(hidden), in_hbm(norm_scale.reshape(d_model // 128, 128)),
+          in_hbm(positions.reshape(1, n_seq)), in_hbm(w_qkv), in_hbm(k_cache.reshape(flat)),
+          in_hbm(v_cache.reshape(flat)))
+
+        part, k_out, v_out, _, _ = pl.pallas_call(
+            functools.partial(attn_kernel, (q_per_kv, head, pitch)),
+            out_shape=(pltpu.VMEM((n_sp, n_rows + 8, head), F32), hbm_cache, hbm_cache, vmem_cache, vmem_cache),
+            in_specs=[SMEM, VMEM, VMEM, VMEM],
+            out_specs=(VMEM, HBM, HBM, VMEM, VMEM),
+            input_output_aliases={2: 3, 3: 4},
+            scratch_shapes=[DMA((2, n_sp))],
+            compiler_params=pltpu.CompilerParams(vmem_limit_bytes=4 * MIB),
             name='attn',
-        )(positions, qkv, k_cache.reshape(flat), v_cache.reshape(flat))
+        )(positions, qkv, k_now, v_now)
 
         nx = n_sp // CORES
         cols = d_model // (CORES * n_tp)
@@ -383,7 +408,7 @@
         h_out = pl.pallas_call(
             functools.partial(out_kernel, (n_tp, n_sp, heads)),
             out_shape=jax.ShapeDtypeStruct((n_seq, d_model), F32),
-            in_specs=[VMEM, ANY, ANY],
+            in_specs=[VMEM, HBM, HBM],
             out_specs=VMEM,
             scratch_shapes=[
                 pltpu.VMEM((n_sp, n_rows + 8, head), F32),
@@ -400,9 +425,9 @@
                 DMA((2, n_tp, nx)), DMA((2, n_tp, nx)),
             ],
             compiler_params=pltpu.CompilerParams(
-                collective_id=1, has_side_effects=True, vmem_limit_bytes=VMEM_LIMIT),
+                collective_id=1, has_side_effects=True, vmem_limit_bytes=28 * MIB),
             name='outproj',
-        )(part, hidden, w_out)
+        )(part, in_hbm(hidden), in_hbm(w_out))
         return h_out.astype(BF16), k_out.reshape(k_cache.shape), v_out.reshape(v_cache.shape)
 
     return jax.shard_map(

time: 63.9 us -> 60.9 us (0.953)
  other arithmetic: 2.67 us -> 1.08 us
  local copies, waits for them, and re-layouts: 1.35 us -> 0.01 us
    pallas_call x2, Pallas kernels: 21.9 us -> 24.1 us  [the longest x1 18.7 us: local_step(): pl.pallas_call(functools.partial(qkv_kernel, (q_per_kv, head, pitch)), ou...]
    pallas_call x1, Pallas kernels: 37 us -> 34.9 us  [local_step(): pl.pallas_call(functools.partial(out_kernel, (n_tp, n_sp, heads)), out_sh...]
    convert_element_type x1, other arithmetic: 2.67 us -> 1.08 us  [local_step(): h_out.astype(BF16)]
    reshape x1 -> x0, local copies, waits for them, and re-layouts: 1.35 us -> none  [local_step(): norm_scale.reshape(1, d_model)]
where the time goes in v4:
time: 60.9 us; the launch traced here: 60.8 us
  Pallas kernels  59 us (97%)
  other arithmetic  1.08 us (2%)
  between operations  0.67 us (1%)
    pallas_call x1, Pallas kernels, local_step(): pl.pallas_call(functools.partial(out_kernel, (n_tp, n_sp, heads)), out_sh...  34.9 us
    pallas_call x1, Pallas kernels, local_step(): pl.pallas_call(functools.partial(qkv_kernel, (q_per_kv, head, pitch)), ou...  18.7 us
    pallas_call x1, Pallas kernels, local_step(): pl.pallas_call(functools.partial(attn_kernel, (q_per_kv, head, pitch)), o...  5.44 us

profile of v4, /device:TPU:97, one launch (start us, length us, event | category | flops | bytes accessed | tf_op | source)
XLA Modules:
  0.0 60.8 jit_solution(16301012858671194328)
XLA Ops:
  0.6 0.0 copy-start
  0.6 18.7 %qkv.1 = (f32[2,720,128]{2,1,0:T(8,128)S(1)}, bf16[64,256,128]{2,1,0:T(8,128)(2,1)S(1)}, bf16[64,256,128]{2,1,0:T(8,128)(2,1)S(1)}) custom-call(bf16[64,8192]{1,0:T(8,128)(2,1)} %h_ref.1, bf16[64,128]{1,0:T(8,128)(2,1)} %bitcast.9, s32[1,64]{1,0:T(1,128)} %bitcast.6, bf16[8192,2560]{1,0:T(8,128)(2,1)} %w_ref.2, bf16[64,256,128]{2,1,0:T(8,128)(2,1)} %bitcast.7, ...), custom_call_target="tpu_custom_call" | custom-call | tf_op jit(solution)/shard_map/qkv/pallas_call | solution.py:372
  19.3 0.0 copy-done
  19.3 5.4 %attn.1 = (f32[8,136,128]{2,1,0:T(8,128)S(1)}, bf16[64,256,128]{2,1,0:T(8,128)(2,1)}, bf16[64,256,128]{2,1,0:T(8,128)(2,1)}, bf16[64,256,128]{2,1,0:T(8,128)(2,1)S(1)}, bf16[64,256,128]{2,1,0:T(8,128)(2,1)S(1)}) custom-call(s32[64]{0:T(128)S(1)} %copy-done, ...), custom_call_target="tpu_custom_call", output_to_operand_aliasing={{3}: (2, {}), {4}: (3, {})} | custom-call | tf_op jit(solution)/shard_map/attn/pallas_call | solution.py:394
  24.8 34.9 %outproj.1 = f32[64,8192]{1,0:T(8,128)S(1)} custom-call(f32[8,136,128]{2,1,0:T(8,128)S(1)} %get-tuple-element.12.o_ref, bf16[64,8192]{1,0:T(8,128)(2,1)} %h_ref.1, bf16[2048,8192]{1,0:T(8,128)(2,1)} %w_ref.3), custom_call_target="tpu_custom_call" | custom-call | tf_op jit(solution)/shard_map/outproj/pallas_call | solution.py:408
  59.7 1.1 %convert_element_type.3 = bf16[64,8192]{1,0:T(8,128)(2,1)} convert(f32[64,8192]{1,0:T(8,128)S(1)} %outproj.1) | non-fusion elementwise | flops 524288 | bytes 3145728 | tf_op jit(solution)/shard_map/convert_element_type | solution.py:431
Async XLA Ops:
  0.6 18.7 %copy-start = (s32[64]{0:T(128)S(1)}, s32[64]{0:T(128)}, u32[]{:S(2)}) copy-start(s32[64]{0:T(128)} %pos_ref.1) | copy-start | bytes 772

commit v5 on v4

--- a/solution.py
+++ b/solution.py
@@ -15,6 +15,7 @@
 VMEM = pl.BlockSpec(memory_space=pltpu.VMEM)
 SMEM = pl.BlockSpec(memory_space=pltpu.SMEM)
 CORES = 2
+CACHE_STEP = 4
 MIB = 1024 * 1024
 
 
@@ -34,18 +35,17 @@
 
 
 def qkv_kernel(dims, h_hbm, scale_hbm, pos_hbm, w_ref, k_hbm, v_hbm, out_ref, kbuf, vbuf, h_ref, scale_ref, pos_ref,
-               wbuf, u_ref, gain, hsem, wsem, csem, s_part, r_part):
+               wbuf, u_ref, acc, gain, hsem, wsem, csem, s_part, r_part):
     n_seq, d_model = h_ref.shape
     q_per_kv, head, pitch = dims
-    n_blk, n_half, blk, cols = wbuf.shape
-    grp = (q_per_kv + 2) * head
+    n_blk, blk, grp = wbuf.shape
     s = lax.axis_index('sp')
     core = lax.rem(s, CORES)
     partner = s + 1 - 2 * core
 
-    def wload(i, k):
+    def wload(i):
         return pltpu.make_async_copy(
-            w_ref.at[pl.ds(k * blk, blk), ds(core * grp + i * cols, cols, 128)], wbuf.at[i, k], wsem.at[i, k])
+            w_ref.at[ds(i * blk, blk, blk), ds(core * grp, grp, 128)], wbuf.at[i], wsem.at[i])
 
     loads = [
         pltpu.make_async_copy(src, dst, hsem.at[i])
@@ -57,8 +57,7 @@
     for load in loads:
         load.start()
     for i in range(n_blk):
-        for k in range(n_half):
-            wload(i, k).start()
+        wload(i).start()
     barrier = pltpu.get_barrier_semaphore()
     pl.semaphore_signal(barrier, inc=1, device_id={'sp': partner}, device_id_type=MESH)
     for load in loads:
@@ -102,27 +101,29 @@
         ref = out_ref.at[core, pl.ds(j * pitch, n_seq)]
         return rcopy(ref, ref, s_part.at[j], r_part.at[j], sp=partner)
 
-    for i in range(n_blk):
-        tot = None
-        for k in range(n_half):
-            wload(i, k).wait()
-            prod = jnp.dot(u_ref[:, k * blk:(k + 1) * blk], wbuf[i, k], preferred_element_type=F32)
-            tot = prod if tot is None else tot + prod
-        per_blk = cols // head
-        for t in range(per_blk):
-            j = i * per_blk + t
-            val = jnp.clip(tot[:, t * head:(t + 1) * head].astype(BF16), -8.0, 8.0).astype(F32)
-            if j < q_per_kv + 1:
-                val = (val * cos_t + pltpu.roll(val, half, 1) * sin_t).astype(BF16).astype(F32)
-            out_ref[core, j * pitch:j * pitch + n_seq, :] = val
-        if i == 0:
-            pl.semaphore_wait(barrier, 1)
-        for t in range(per_blk):
-            psend(i * per_blk + t).start()
-        if i == 1:
+    acc[...] = jnp.zeros_like(acc)
+
+    def mm(i, carry):
+        wload(i).wait()
+
+        @pl.when(i == CACHE_STEP)
+        def _():
             caches[0].start()
-        if i == 2:
             caches[1].start()
+
+        acc[...] += jnp.dot(u_ref[:, ds(i * blk, blk, blk)], wbuf[i], preferred_element_type=F32)
+        return carry
+
+    lax.fori_loop(0, n_blk, mm, 0)
+    pl.semaphore_wait(barrier, 1)
+    for j in range(q_per_kv + 2):
+        val = jnp.clip(acc[:, j * head:(j + 1) * head].astype(BF16), -8.0, 8.0).astype(F32)
+        if j < q_per_kv + 1:
+            val = (val * cos_t + pltpu.roll(val, half, 1) * sin_t).astype(BF16).astype(F32)
+        out_ref[core, j * pitch:j * pitch + n_seq, :] = val
+        if j > 0:
+            psend(j - 1).start()
+    psend(q_per_kv + 1).start()
     for j in range(q_per_kv + 2):
         psend(j).wait()
     for cp in caches:
@@ -361,7 +362,7 @@
         q_per_kv = w_qkv.shape[1] // (kv_local * head) - 2
         heads = kv_local * q_per_kv
         grp_cols = (q_per_kv + 2) * head
-        n_blk, n_half = (q_per_kv + 2) // 2, 2
+        n_blk = 8
         pitch = n_seq + 8
         per = n_seq // n_sp
         n_rows = per * heads
@@ -378,10 +379,11 @@
                 pltpu.VMEM(hidden.shape, BF16),
                 pltpu.VMEM((d_model // 128, 128), BF16),
                 pltpu.VMEM((1, n_seq), jnp.int32),
-                pltpu.VMEM((n_blk, n_half, d_model // n_half, grp_cols // n_blk), BF16),
+                pltpu.VMEM((n_blk, d_model // n_blk, grp_cols), BF16),
                 pltpu.VMEM((n_seq, d_model), BF16),
+                pltpu.VMEM((n_seq, grp_cols), F32),
                 pltpu.VMEM((d_model // 128, 128), F32),
-                DMA((3,)), DMA((n_blk, n_half)), DMA((2,)),
+                DMA((3,)), DMA((n_blk,)), DMA((2,)),
                 DMA((q_per_kv + 2,)), DMA((q_per_kv + 2,)),
             ],
             compiler_params=pltpu.CompilerParams(

time: 60.9 us -> 59.2 us (0.972)
  Pallas kernels: 59 us -> 57.4 us
    pallas_call x1, Pallas kernels: 18.7 us -> 16.7 us  [local_step(): pl.pallas_call(functools.partial(qkv_kernel, (q_per_kv, head, pitch)), ou...]
where the time goes in v5:
time: 59.2 us
  Pallas kernels  57.4 us (97%)
  other arithmetic  1.08 us (2%)
  between operations  0.67 us (1%)
    pallas_call x1, Pallas kernels, local_step(): pl.pallas_call(functools.partial(out_kernel, (n_tp, n_sp, heads)), out_sh...  35.3 us
    pallas_call x1, Pallas kernels, local_step(): pl.pallas_call(functools.partial(qkv_kernel, (q_per_kv, head, pitch)), ou...  16.7 us
    pallas_call x1, Pallas kernels, local_step(): pl.pallas_call(functools.partial(attn_kernel, (q_per_kv, head, pitch)), o...  5.44 us

profile of v5, /device:TPU:97, one launch (start us, length us, event | category | flops | bytes accessed | tf_op | source)
XLA Modules:
  0.0 59.2 jit_solution(7447617428261483259)
XLA Ops:
  0.6 0.0 copy-start
  0.6 16.7 %qkv.1 = (f32[2,720,128]{2,1,0:T(8,128)S(1)}, bf16[64,256,128]{2,1,0:T(8,128)(2,1)S(1)}, bf16[64,256,128]{2,1,0:T(8,128)(2,1)S(1)}) custom-call(bf16[64,8192]{1,0:T(8,128)(2,1)} %h_ref.1, bf16[64,128]{1,0:T(8,128)(2,1)} %bitcast.9, s32[1,64]{1,0:T(1,128)} %bitcast.6, bf16[8192,2560]{1,0:T(8,128)(2,1)} %w_ref.2, bf16[64,256,128]{2,1,0:T(8,128)(2,1)} %bitcast.7, ...), custom_call_target="tpu_custom_call" | custom-call | tf_op jit(solution)/shard_map/qkv/pallas_call | solution.py:373
  17.3 0.0 copy-done
  17.4 5.4 %attn.1 = (f32[8,136,128]{2,1,0:T(8,128)S(1)}, bf16[64,256,128]{2,1,0:T(8,128)(2,1)}, bf16[64,256,128]{2,1,0:T(8,128)(2,1)}, bf16[64,256,128]{2,1,0:T(8,128)(2,1)S(1)}, bf16[64,256,128]{2,1,0:T(8,128)(2,1)S(1)}) custom-call(s32[64]{0:T(128)S(1)} %copy-done, ...), custom_call_target="tpu_custom_call", output_to_operand_aliasing={{3}: (2, {}), {4}: (3, {})} | custom-call | tf_op jit(solution)/shard_map/attn/pallas_call | solution.py:396
  22.8 35.3 %outproj.1 = f32[64,8192]{1,0:T(8,128)S(1)} custom-call(f32[8,136,128]{2,1,0:T(8,128)S(1)} %get-tuple-element.12.o_ref, bf16[64,8192]{1,0:T(8,128)(2,1)} %h_ref.1, bf16[2048,8192]{1,0:T(8,128)(2,1)} %w_ref.3), custom_call_target="tpu_custom_call" | custom-call | tf_op jit(solution)/shard_map/outproj/pallas_call | solution.py:410
  58.1 1.1 %convert_element_type.3 = bf16[64,8192]{1,0:T(8,128)(2,1)} convert(f32[64,8192]{1,0:T(8,128)S(1)} %outproj.1) | non-fusion elementwise | flops 524288 | bytes 3145728 | tf_op jit(solution)/shard_map/convert_element_type | solution.py:433
Async XLA Ops:
  0.6 16.7 %copy-start = (s32[64]{0:T(128)S(1)}, s32[64]{0:T(128)}, u32[]{:S(2)}) copy-start(s32[64]{0:T(128)} %pos_ref.1) | copy-start | bytes 772

commit v6 on v5

v6 whole, which is shorter than its diff:
```python
import functools
import math

import jax
import jax.numpy as jnp
from jax import lax
from jax.experimental import pallas as pl
from jax.experimental.pallas import tpu as pltpu
from jax.sharding import PartitionSpec as P

MESH = pl.DeviceIdType.MESH
F32 = jnp.float32
BF16 = jnp.bfloat16
HBM = pl.BlockSpec(memory_space=pltpu.HBM)
VMEM = pl.BlockSpec(memory_space=pltpu.VMEM)
SMEM = pl.BlockSpec(memory_space=pltpu.SMEM)
CORES = 2
CACHE_STEP = 4
MIB = 1024 * 1024


def in_hbm(val):
    return pltpu.with_memory_space_constraint(val, pltpu.HBM)


def ds(start, size, align):
    return pl.ds(pl.multiple_of(start, align), size)


def rcopy(src, dst, send_sem, recv_sem, **where):
    return pltpu.make_async_remote_copy(
        src_ref=src, dst_ref=dst, send_sem=send_sem, recv_sem=recv_sem,
        device_id=where, device_id_type=MESH,
    )


def main_kernel(dims, pos_smem, h_hbm, scale_hbm, pos_hbm, w_ref, k_hbm, v_hbm, wo_ref, out_ref, kbuf, vbuf, res_ref,
                h_ref, scale_ref, pos_ref, wbuf, u_ref, acc, gain, o_ref, rbuf, abuf, attn, lhs, wobuf, pbuf, ybuf, hbuf,
                hsem, wsem, csem, s_part, r_part, wosem, hosem, rs_s, rs_r, ab_s, ab_r, y_s, y_r, a_s, a_r, b_s, b_r,
                d_s, d_r):
    n_seq, d_model = h_ref.shape
    q_per_kv, head, pitch, n_tp, n_sp = dims
    n_blk, blk, grp = wbuf.shape
    groups = out_ref.shape[0]
    heads = groups * q_per_kv
    rows2 = kbuf.shape[1]
    n_grp = rows2 // groups
    nx = n_sp // CORES
    y = lax.axis_index('tp')
    s = lax.axis_index('sp')
    core = lax.rem(s, CORES)
    x = s // CORES
    partner = s + 1 - 2 * core
    n_rows = attn.shape[1]
    per = n_rows // heads
    cols = wobuf.shape[2]
    seqs = CORES * per
    base = s * n_grp

    def yat(d):
        return lax.rem(y + d, n_tp)

    def xat(d):
        return lax.rem(x + d, nx) * CORES + core

    def wload(i):
        return pltpu.make_async_copy(
            w_ref.at[ds(i * blk, blk, blk), ds(core * grp, grp, 128)], wbuf.at[i], wsem.at[i])

    def wcopy(j):
        return pltpu.make_async_copy(
            wo_ref.at[:, ds((core * n_tp + yat(j)) * cols, cols, cols)], wobuf.at[j], wosem.at[j])

    def chunk_of(d):
        return lax.rem(s + d, n_sp)

    def ccopy(d, which):
        src, dst = ((k_hbm, kbuf), (v_hbm, vbuf))[which]
        cut = pl.ds(chunk_of(d) * per, per)
        return pltpu.make_async_copy(src.at[cut], dst.at[cut], csem.at[which, d])

    def owner(t):
        return 1 + (t + n_sp // 2 - 2) % (n_sp - 1)

    hcopy = pltpu.make_async_copy(
        h_hbm.at[ds(x * seqs, seqs, seqs), ds((core * n_tp + y) * cols, cols, cols)], hbuf, hosem)
    order = [d for d in range(1, n_tp)] + [0]
    loads = [
        pltpu.make_async_copy(src, dst, hsem.at[i])
        for i, (src, dst) in enumerate(((h_hbm, h_ref), (scale_hbm, scale_ref), (pos_hbm, pos_ref)))
    ]
    for load in loads:
        load.start()
    for i in range(n_blk):
        wload(i).start()
    barrier = pltpu.get_barrier_semaphore()
    for d in range(1, n_sp):
        pl.semaphore_signal(barrier, inc=1, device_id={'sp': lax.rem(s + d, n_sp)}, device_id_type=MESH)
    for d in range(1, n_tp):
        pl.semaphore_signal(barrier, inc=1, device_id={'tp': yat(d)}, device_id_type=MESH)
    for load in loads:
        load.wait()

    lanes = 128
    zero = jnp.zeros((n_seq, lanes), F32)

    def add_sum(i, tot):
        return tot + h_ref[:, ds(i * lanes, lanes, lanes)].astype(F32)

    mean = jnp.sum(lax.fori_loop(0, d_model // lanes, add_sum, zero, unroll=8), axis=1, keepdims=True) / d_model

    def add_sq(i, tot):
        cent = h_ref[:, ds(i * lanes, lanes, lanes)].astype(F32) - mean
        return tot + cent * cent

    var = jnp.sum(lax.fori_loop(0, d_model // lanes, add_sq, zero, unroll=8), axis=1, keepdims=True) / d_model
    inv = lax.rsqrt(var + 1e-5)

    gain[...] = scale_ref[...].astype(F32)

    def norm(i, carry):
        cut = ds(i * lanes, lanes, lanes)
        cent = h_ref[:, cut].astype(F32) - mean
        u_ref[:, cut] = (cent * inv * gain[pl.ds(i, 1), :]).astype(BF16)
        return carry

    lax.fori_loop(0, d_model // lanes, norm, 0, unroll=8)

    eye = lax.broadcasted_iota(jnp.int32, (n_seq, n_seq), 0) == lax.broadcasted_iota(jnp.int32, (n_seq, n_seq), 1)
    pos_col = jnp.sum(jnp.where(eye, pos_ref[...].astype(F32), 0.0), axis=1, keepdims=True)
    lane = lax.broadcasted_iota(jnp.int32, (n_seq, head), 1)
    half = head // 2
    inv_freq = jnp.exp(lax.rem(lane, half).astype(F32) * (-2.0 * math.log(500000.0) / head))
    angle = pos_col * inv_freq
    cos_t = jnp.cos(angle)
    sin_t = jnp.where(lane < half, -jnp.sin(angle), jnp.sin(angle))

    def psend(j):
        ref = out_ref.at[core, pl.ds(j * pitch, n_seq)]
        return rcopy(ref, ref, s_part.at[j], r_part.at[j], sp=partner)

    acc[...] = jnp.zeros_like(acc)

    def mm(i, carry):
        wload(i).wait()

        @pl.when(i == CACHE_STEP)
        def _():
            for d in [owner(t) for t in range(n_sp - 1)] + [0]:
                ccopy(d, 0).start()
                ccopy(d, 1).start()

        acc[...] += jnp.dot(u_ref[:, ds(i * blk, blk, blk)], wbuf[i], preferred_element_type=F32)
        return carry

    lax.fori_loop(0, n_blk, mm, 0)
    pl.semaphore_wait(barrier, n_sp + n_tp - 2)
    for j in order:
        wcopy(j).start()
    hcopy.start()
    for j in range(q_per_kv + 2):
        val = jnp.clip(acc[:, j * head:(j + 1) * head].astype(BF16), -8.0, 8.0).astype(F32)
        if j < q_per_kv + 1:
            val = (val * cos_t + pltpu.roll(val, half, 1) * sin_t).astype(BF16).astype(F32)
        out_ref[core, j * pitch:j * pitch + n_seq, :] = val
        if j > 0:
            psend(j - 1).start()
    psend(q_per_kv + 1).start()
    colj = lax.broadcasted_iota(jnp.int32, (heads, rows2), 1)
    rown = lax.broadcasted_iota(jnp.int32, (heads, rows2), 0)
    same = lax.rem(colj, groups) == rown // q_per_kv
    eye = lax.broadcasted_iota(jnp.int32, (n_rows, n_rows), 0) == lax.broadcasted_iota(jnp.int32, (n_rows, n_rows), 1)
    for j in range(q_per_kv + 2):
        psend(j).wait_recv()

    def rs(d):
        to = chunk_of(d)
        return rcopy(o_ref.at[d], rbuf.at[d], rs_s.at[d], rs_r.at[d], sp=to)

    def attend(d):
        i = chunk_of(d)
        ccopy(d, 0).wait()
        ccopy(d, 1).wait()
        scores, fresh, vals = [], [], []
        for t in range(per):
            b = i * per + t
            rel = pos_smem[b] - base
            rows = [
                jnp.concatenate([
                    jnp.broadcast_to(out_ref[g, pl.ds(off * pitch + b, 1), :], (q_per_kv, head)) for g in range(groups)
                ], axis=0) for off in (q_per_kv, q_per_kv + 1)
            ]
            q = jnp.concatenate([out_ref[g, pl.ds(b, q_per_kv, stride=pitch), :] for g in range(groups)], axis=0)
            sc = lax.dot_general(q.astype(BF16), kbuf[b], (((1,), (1,)), ((), ())), preferred_element_type=F32)
            ok = jnp.logical_and(same, colj < groups * rel)
            scores.append(jnp.where(ok, sc * (head ** -0.5), -1e30))
            own = jnp.sum(q * rows[0], axis=1, keepdims=True) * (head ** -0.5)
            at = jnp.full((heads, 1), rel, jnp.int32)
            fresh.append(jnp.where(jnp.logical_and(at >= 0, at < n_grp), own, -1e30))
            vals.append(rows[1])
        sc = jnp.concatenate(scores, axis=0)
        own = jnp.concatenate(fresh, axis=0)
        top = jnp.maximum(jnp.max(sc, axis=1, keepdims=True), own)
        wt = jnp.exp(sc - top)
        own = jnp.exp(own - top)
        tot = jnp.sum(wt, axis=1, keepdims=True) + own
        wt = wt.astype(BF16)
        own = own.astype(BF16).astype(F32)
        for t in range(per):
            cut = slice(t * heads, (t + 1) * heads)
            o_ref[d, cut, :] = jnp.dot(
                wt[cut], vbuf[i * per + t], preferred_element_type=F32) + own[cut] * vals[t]
        top_row = jnp.sum(jnp.where(eye, top, 0.0), axis=0, keepdims=True)
        tot_row = jnp.sum(jnp.where(eye, tot, 0.0), axis=0, keepdims=True)
        pad = jnp.zeros((6, n_rows), F32)
        o_ref[d, n_rows:n_rows + 8, :] = jnp.concatenate([top_row, tot_row, pad], axis=0)

    def sweep(t, carry):
        d = owner(t)
        attend(d)
        rs(d).start()
        return carry

    lax.fori_loop(0, n_sp - 1, sweep, 0)
    attend(0)
    parts = [o_ref.at[0]]
    for d in range(1, n_sp):
        rs(d).wait_recv()
        parts.append(rbuf.at[d])
    tops = [p[n_rows:n_rows + 1, :] for p in parts]
    sums = [p[n_rows + 1:n_rows + 2, :] for p in parts]
    top = functools.reduce(jnp.maximum, tops)
    facs = [jnp.exp(t - top) for t in tops]
    tot = functools.reduce(jnp.add, [f * l for f, l in zip(facs, sums)])
    fac = jnp.concatenate([f / tot for f in facs], axis=0)
    pad = jnp.zeros((n_rows - n_sp, n_rows), F32)
    fac = jnp.transpose(jnp.concatenate([fac, pad], axis=0))
    val = parts[0][0:n_rows, :] * fac[:, 0:1]
    for j in range(1, n_sp):
        val = val + parts[j][0:n_rows, :] * fac[:, j:j + 1]
    attn[0] = val

    swap = rcopy(attn.at[0], abuf.at[core], ab_s, ab_r, sp=partner)
    swap.start()
    abuf[core] = val
    swap.wait()
    flat = abuf.reshape(CORES * n_rows, head)
    for n in range(heads):
        lhs[:, n * head:(n + 1) * head] = flat[pl.ds(n, seqs, stride=heads), :].astype(BF16)

    def ysend(d):
        return rcopy(pbuf.at[d], ybuf.at[d], y_s.at[d], y_r.at[d], tp=yat(d))

    def proj(j):
        wcopy(j).wait()
        pbuf[j] = jnp.dot(lhs[...], wobuf[j], preferred_element_type=F32)

    for j in order:
        proj(j)
        if j:
            ysend(j).start()
    hcopy.wait()
    tot = pbuf[0]
    for d in range(1, n_tp):
        ysend(d).wait_recv()
        tot = tot + ybuf[d]
    res_ref[ds(x * seqs, seqs, seqs), ds((core * n_tp + y) * cols, cols, cols)] = hbuf[...].astype(F32) + tot

    def block(dy, dx, part):
        by = lax.rem(y + n_tp - dy, n_tp)
        bx = lax.rem(x + nx - dx, nx)
        return res_ref.at[ds(bx * seqs + part * per, per, per), ds((core * n_tp + by) * cols, cols, cols)]

    sends = []

    def go(dy, dx, part, sems, where, ty, tx):
        ref = block(dy, dx, part)
        cp = rcopy(ref, ref, sems[0].at[ty, tx], sems[1].at[ty, tx], **where)
        cp.start()
        sends.append(cp)

    def fwd(dy, dx, part):
        if part == 0 and dx == 0:
            for e in range(1, nx):
                go(dy, 0, 0, (a_s, a_r), {'sp': xat(e)}, dy, e)
        if part == 1 and dy == 0:
            for e in range(1, n_tp):
                go(0, dx, 1, (b_s, b_r), {'tp': yat(e)}, e, dx)
        ref = block(dy, dx, part)
        cp = rcopy(ref, ref, d_s.at[part, dy, dx], d_r.at[part, dy, dx], sp=partner)
        cp.start()
        sends.append(cp)

    for e in range(1, n_tp):
        go(0, 0, 0, (a_s, a_r), {'tp': yat(e)}, e, 0)
    for e in range(1, nx):
        go(0, 0, 1, (b_s, b_r), {'sp': xat(e)}, 0, e)
    fwd(0, 0, 0)
    fwd(0, 0, 1)

    def arrive(dy, dx, part):
        ref = block(dy, dx, part)
        r = (a_r, b_r)[part].at[dy, dx]
        q = (a_s, b_s)[part].at[dy, dx]
        rcopy(ref, ref, q, r, sp=partner).wait_recv()
        fwd(dy, dx, part)

    for e in range(1, max(n_tp, nx)):
        if e < n_tp:
            arrive(e, 0, 0)
        if e < nx:
            arrive(0, e, 1)
    for dy in range(n_tp):
        for e in range(1, nx):
            arrive(dy, e, 0)
    for dx in range(nx):
        for e in range(1, n_tp):
            arrive(e, dx, 1)
    for part in range(2):
        for dy in range(n_tp):
            for dx in range(nx):
                by = lax.rem(y + n_tp - dy, n_tp)
                bx = lax.rem(x + nx - dx, nx)
                ref = res_ref.at[ds(bx * seqs + part * per, per, per),
                                 ds(((1 - core) * n_tp + by) * cols, cols, cols)]
                rcopy(ref, ref, d_s.at[part, dy, dx], d_r.at[part, dy, dx], sp=partner).wait_recv()
    for cp in sends:
        cp.wait_send()
    for d in range(1, n_sp):
        rs(d).wait_send()
    for d in range(1, n_tp):
        ysend(d).wait_send()
    for j in range(q_per_kv + 2):
        psend(j).wait_send()


def write_kernel(dims, pos_ref, qkv_ref, res_ref, k_ref, v_ref, h_out, ko_ref, vo_ref, kbuf, vbuf, hbuf, osem, hsem):
    q_per_kv, head, pitch, n_ch = dims
    n_seq, rows2, _ = kbuf.shape
    groups = qkv_ref.shape[0]
    n_grp = rows2 // groups
    per = n_seq // n_ch
    base = lax.axis_index('sp') * n_grp
    tile = 8 * groups
    trow = lax.broadcasted_iota(jnp.int32, (tile, head), 0)

    def bulk(i, which):
        src, dst = ((kbuf, ko_ref), (vbuf, vo_ref))[which]
        cut = pl.ds(i * per, per)
        return pltpu.make_async_copy(src.at[cut], dst.at[cut], osem.at[which, i])

    def hwrite(i):
        cut = pl.ds(i * 16, 16)
        return pltpu.make_async_copy(hbuf.at[cut], h_out.at[cut], hsem.at[i])

    def step(i, carry):
        for t in range(per):
            b = i * per + t
            rel = pos_ref[b] - base
            here = jnp.logical_and(rel >= 0, rel < n_grp)
            at = jnp.clip(rel, 0, n_grp - 1)
            cut = ds((at // 8) * tile, tile, tile)
            hit = jnp.logical_and(trow // groups == at % 8, here)
            for src, buf, off in ((k_ref, kbuf, q_per_kv * pitch), (v_ref, vbuf, (q_per_kv + 1) * pitch)):
                new = qkv_ref[0, pl.ds(off + b, 1), :]
                for g in range(1, groups):
                    new = jnp.where(trow % groups == g, qkv_ref[g, pl.ds(off + b, 1), :], new)
                buf[b, cut, :] = jnp.where(hit, new, src[b, cut, :].astype(F32)).astype(BF16)

        @pl.when(i > 0)
        def _():
            bulk(i - 1, 0).start()
            bulk(i - 1, 1).start()

        return carry

    lax.fori_loop(0, n_ch, step, 0)
    bulk(n_ch - 1, 0).start()
    bulk(n_ch - 1, 1).start()
    n_h = n_seq // 16
    for i in range(n_h):
        hbuf[i * 16:(i + 1) * 16, :] = res_ref[i * 16:(i + 1) * 16, :].astype(BF16)
        if i > 0:
            hwrite(i - 1).start()
    hwrite(n_h - 1).start()
    for i in range(n_ch):
        bulk(i, 0).wait()
        bulk(i, 1).wait()
    for i in range(n_h):
        hwrite(i).wait()


def solution(mesh):
    n_tp, n_sp = mesh.shape['tp'], mesh.shape['sp']
    cache_spec = P('dp', 'sp', 'tp', None)
    DMA = pltpu.SemaphoreType.DMA

    def local_step(hidden, norm_scale, w_qkv, w_out, k_cache, v_cache, positions):
        n_seq, seq_local, kv_local, head = k_cache.shape
        d_model = hidden.shape[1]
        q_per_kv = w_qkv.shape[1] // (kv_local * head) - 2
        heads = kv_local * q_per_kv
        grp_cols = (q_per_kv + 2) * head
        n_blk = 8
        pitch = n_seq + 8
        per = n_seq // n_sp
        n_rows = per * heads
        flat = (n_seq, seq_local * kv_local, head)
        vmem_cache = pltpu.VMEM(flat, BF16)
        hbm_cache = jax.ShapeDtypeStruct(flat, BF16)

        nx = n_sp // CORES
        cols = d_model // (CORES * n_tp)
        depth = w_out.shape[0]
        qkv, k_now, v_now, res = pl.pallas_call(
            functools.partial(main_kernel, (q_per_kv, head, pitch, n_tp, n_sp)),
            out_shape=(pltpu.VMEM((kv_local, pitch * (q_per_kv + 2), head), F32), vmem_cache, vmem_cache,
                       pltpu.VMEM((n_seq, d_model), F32)),
            in_specs=[SMEM] + [HBM] * 7,
            out_specs=(VMEM,) * 4,
            scratch_shapes=[
                pltpu.VMEM(hidden.shape, BF16),
                pltpu.VMEM((d_model // 128, 128), BF16),
                pltpu.VMEM((1, n_seq), jnp.int32),
                pltpu.VMEM((n_blk, d_model // n_blk, grp_cols), BF16),
                pltpu.VMEM((n_seq, d_model), BF16),
                pltpu.VMEM((n_seq, grp_cols), F32),
                pltpu.VMEM((d_model // 128, 128), F32),
                pltpu.VMEM((n_sp, n_rows + 8, head), F32),
                pltpu.VMEM((n_sp, n_rows + 8, head), F32),
                pltpu.VMEM((CORES, n_rows, head), F32),
                pltpu.VMEM((1, n_rows, head), F32),
                pltpu.VMEM((CORES * per, depth), BF16),
                pltpu.VMEM((n_tp, depth, cols), BF16),
                pltpu.VMEM((n_tp, CORES * per, cols), F32),
                pltpu.VMEM((n_tp, CORES * per, cols), F32),
                pltpu.VMEM((CORES * per, cols), BF16),
                DMA((3,)), DMA((n_blk,)), DMA((2, n_sp)), DMA((q_per_kv + 2,)), DMA((q_per_kv + 2,)),
                DMA((n_tp,)), DMA,
                DMA((n_sp,)), DMA((n_sp,)), DMA, DMA, DMA((n_tp,)), DMA((n_tp,)),
                DMA((n_tp, nx)), DMA((n_tp, nx)), DMA((n_tp, nx)), DMA((n_tp, nx)),
                DMA((2, n_tp, nx)), DMA((2, n_tp, nx)),
            ],
            compiler_params=pltpu.CompilerParams(
                collective_id=0, has_side_effects=True, vmem_limit_bytes=46 * MIB),
            name='main',
        )(positions, in_hbm(hidden), in_hbm(norm_scale.reshape(d_model // 128, 128)),
          in_hbm(positions.reshape(1, n_seq)), in_hbm(w_qkv), in_hbm(k_cache.reshape(flat)),
          in_hbm(v_cache.reshape(flat)), in_hbm(w_out))

        h_out, k_out, v_out, _, _ = pl.pallas_call(
            functools.partial(write_kernel, (q_per_kv, head, pitch, n_sp)),
            out_shape=(jax.ShapeDtypeStruct(hidden.shape, BF16), hbm_cache, hbm_cache, vmem_cache, vmem_cache),
            in_specs=[SMEM, VMEM, VMEM, VMEM, VMEM],
            out_specs=(HBM, HBM, HBM, VMEM, VMEM),
            input_output_aliases={3: 3, 4: 4},
            scratch_shapes=[pltpu.VMEM(hidden.shape, BF16), DMA((2, n_sp)), DMA((n_seq // 16,))],
            compiler_params=pltpu.CompilerParams(vmem_limit_bytes=4 * MIB),
            name='write',
        )(positions, qkv, res, k_now, v_now)
        return h_out, k_out.reshape(k_cache.shape), v_out.reshape(v_cache.shape)

    return jax.shard_map(
        local_step,
        mesh=mesh,
        in_specs=(P('dp', None), P(None), P(None, 'tp'), P('tp', None), cache_spec, cache_spec, P('dp')),
        out_specs=(P('dp', None), cache_spec, cache_spec),
        check_vma=False,
    )
```

time: 59.2 us -> 55.8 us (0.943)
  Pallas kernels: 57.4 us -> 55.1 us
  other arithmetic: 1.08 us -> 0 us
    pallas_call x3 -> x2, Pallas kernels: 57.4 us -> 55.1 us  [the longest x1 50.6 us: local_step(): pl.pallas_call(functools.partial(main_kernel, (q_per_kv, head, pitch, n_t...]
    convert_element_type x1 -> x0, other arithmetic: 1.08 us -> none  [local_step(): h_out.astype(BF16)]
where the time goes in v6:
time: 55.8 us; the launch traced here: 55.7 us
  Pallas kernels  55.1 us (99%)
  between operations  0.66 us (1%)
    pallas_call x1, Pallas kernels, local_step(): pl.pallas_call(functools.partial(main_kernel, (q_per_kv, head, pitch, n_t...  50.6 us
    pallas_call x1, Pallas kernels, local_step(): pl.pallas_call(functools.partial(write_kernel, (q_per_kv, head, pitch, n_...  4.46 us

profile of v6, /device:TPU:97, one launch (start us, length us, event | category | flops | bytes accessed | tf_op | source)
XLA Modules:
  0.0 55.7 jit_solution(16340307667524834318)
XLA Ops:
  0.6 0.0 copy-start
  0.6 50.6 %main.1 = (f32[2,720,128]{2,1,0:T(8,128)S(1)}, bf16[64,256,128]{2,1,0:T(8,128)(2,1)S(1)}, bf16[64,256,128]{2,1,0:T(8,128)(2,1)S(1)}, f32[64,8192]{1,0:T(8,128)S(1)}) custom-call(s32[64]{0:T(128)} %pos_ref.1, bf16[64,8192]{1,0:T(8,128)(2,1)} %h_hbm.1, bf16[64,128]{1,0:T(8,128)(2,1)} %bitcast.9, s32[1,64]{1,0:T(1,128)} %bitcast.6, bf16[8192,2560]{1,0:T(8,128)(2,1)} %w_ref.1, ...), custom_call_target="tpu_custom_call" | custom-call | tf_op jit(solution)/shard_map/main/pallas_call | solution.py:415
  51.3 0.0 copy-done
  51.3 4.5 %write.1 = (bf16[64,8192]{1,0:T(8,128)(2,1)}, bf16[64,256,128]{2,1,0:T(8,128)(2,1)}, bf16[64,256,128]{2,1,0:T(8,128)(2,1)}, bf16[64,256,128]{2,1,0:T(8,128)(2,1)S(1)}, bf16[64,256,128]{2,1,0:T(8,128)(2,1)S(1)}) custom-call(s32[64]{0:T(128)S(1)} %copy-done, ...), custom_call_target="tpu_custom_call", output_to_operand_aliasing={{3}: (3, {}), {4}: (4, {})} | custom-call | tf_op jit(solution)/shard_map/write/pallas_call | solution.py:451
Async XLA Ops:
  0.6 50.6 %copy-start = (s32[64]{0:T(128)S(1)}, s32[64]{0:T(128)}, u32[]{:S(2)}) copy-start(s32[64]{0:T(128)} %pos_ref.1) | copy-start | bytes 772

commit v7 on v6

--- a/solution.py
+++ b/solution.py
@@ -15,7 +15,7 @@
 VMEM = pl.BlockSpec(memory_space=pltpu.VMEM)
 SMEM = pl.BlockSpec(memory_space=pltpu.SMEM)
 CORES = 2
-CACHE_STEP = 4
+CACHE_STEP = 10
 MIB = 1024 * 1024
 
 
@@ -34,10 +34,10 @@
     )
 
 
-def main_kernel(dims, pos_smem, h_hbm, scale_hbm, pos_hbm, w_ref, k_hbm, v_hbm, wo_ref, out_ref, kbuf, vbuf, res_ref,
+def main_kernel(dims, pos_flat, h_hbm, scale_hbm, pos_hbm, w_ref, k_hbm, v_hbm, wo_ref, out_ref, kbuf, vbuf, res_ref,
                 h_ref, scale_ref, pos_ref, wbuf, u_ref, acc, gain, o_ref, rbuf, abuf, attn, lhs, wobuf, pbuf, ybuf, hbuf,
                 hsem, wsem, csem, s_part, r_part, wosem, hosem, rs_s, rs_r, ab_s, ab_r, y_s, y_r, a_s, a_r, b_s, b_r,
-                d_s, d_r):
+                d_s, d_r, pos_smem):
     n_seq, d_model = h_ref.shape
     q_per_kv, head, pitch, n_tp, n_sp = dims
     n_blk, blk, grp = wbuf.shape
@@ -84,10 +84,13 @@
 
     hcopy = pltpu.make_async_copy(
         h_hbm.at[ds(x * seqs, seqs, seqs), ds((core * n_tp + y) * cols, cols, cols)], hbuf, hosem)
-    order = [d for d in range(1, n_tp)] + [0]
+    far_tp = sorted(range(1, n_tp), key=lambda d: -min(d, n_tp - d))
+    far_x = sorted(range(1, nx), key=lambda d: -min(d, nx - d))
+    order = far_tp + [0]
     loads = [
         pltpu.make_async_copy(src, dst, hsem.at[i])
-        for i, (src, dst) in enumerate(((h_hbm, h_ref), (scale_hbm, scale_ref), (pos_hbm, pos_ref)))
+        for i, (src, dst) in enumerate(
+            ((h_hbm, h_ref), (scale_hbm, scale_ref), (pos_hbm, pos_ref), (pos_flat, pos_smem)))
     ]
     for load in loads:
         load.start()
@@ -281,19 +284,19 @@
 
     def fwd(dy, dx, part):
         if part == 0 and dx == 0:
-            for e in range(1, nx):
+            for e in far_x:
                 go(dy, 0, 0, (a_s, a_r), {'sp': xat(e)}, dy, e)
         if part == 1 and dy == 0:
-            for e in range(1, n_tp):
+            for e in far_tp:
                 go(0, dx, 1, (b_s, b_r), {'tp': yat(e)}, e, dx)
         ref = block(dy, dx, part)
         cp = rcopy(ref, ref, d_s.at[part, dy, dx], d_r.at[part, dy, dx], sp=partner)
         cp.start()
         sends.append(cp)
 
-    for e in range(1, n_tp):
+    for e in far_tp:
         go(0, 0, 0, (a_s, a_r), {'tp': yat(e)}, e, 0)
-    for e in range(1, nx):
+    for e in far_x:
         go(0, 0, 1, (b_s, b_r), {'sp': xat(e)}, 0, e)
     fwd(0, 0, 0)
     fwd(0, 0, 1)
@@ -305,17 +308,14 @@
         rcopy(ref, ref, q, r, sp=partner).wait_recv()
         fwd(dy, dx, part)
 
-    for e in range(1, max(n_tp, nx)):
-        if e < n_tp:
-            arrive(e, 0, 0)
-        if e < nx:
-            arrive(0, e, 1)
-    for dy in range(n_tp):
-        for e in range(1, nx):
-            arrive(dy, e, 0)
-    for dx in range(nx):
-        for e in range(1, n_tp):
-            arrive(e, dx, 1)
+    def hops(item):
+        dy, dx, part = item
+        first = dx == 0 if part == 0 else dy == 0
+        return (not first, min(dy, n_tp - dy) + min(dx, nx - dx), dy + dx)
+
+    due = [(dy, dx, part) for dy in range(n_tp) for dx in range(nx) for part in range(2) if dy + dx > 0]
+    for dy, dx, part in sorted(due, key=hops):
+        arrive(dy, dx, part)
     for part in range(2):
         for dy in range(n_tp):
             for dx in range(nx):
@@ -401,7 +401,7 @@
         q_per_kv = w_qkv.shape[1] // (kv_local * head) - 2
         heads = kv_local * q_per_kv
         grp_cols = (q_per_kv + 2) * head
-        n_blk = 8
+        n_blk = 16
         pitch = n_seq + 8
         per = n_seq // n_sp
         n_rows = per * heads
@@ -416,7 +416,7 @@
             functools.partial(main_kernel, (q_per_kv, head, pitch, n_tp, n_sp)),
             out_shape=(pltpu.VMEM((kv_local, pitch * (q_per_kv + 2), head), F32), vmem_cache, vmem_cache,
                        pltpu.VMEM((n_seq, d_model), F32)),
-            in_specs=[SMEM] + [HBM] * 7,
+            in_specs=[HBM] * 8,
             out_specs=(VMEM,) * 4,
             scratch_shapes=[
                 pltpu.VMEM(hidden.shape, BF16),
@@ -435,16 +435,17 @@
                 pltpu.VMEM((n_tp, CORES * per, cols), F32),
                 pltpu.VMEM((n_tp, CORES * per, cols), F32),
                 pltpu.VMEM((CORES * per, cols), BF16),
-                DMA((3,)), DMA((n_blk,)), DMA((2, n_sp)), DMA((q_per_kv + 2,)), DMA((q_per_kv + 2,)),
+                DMA((4,)), DMA((n_blk,)), DMA((2, n_sp)), DMA((q_per_kv + 2,)), DMA((q_per_kv + 2,)),
                 DMA((n_tp,)), DMA,
                 DMA((n_sp,)), DMA((n_sp,)), DMA, DMA, DMA((n_tp,)), DMA((n_tp,)),
                 DMA((n_tp, nx)), DMA((n_tp, nx)), DMA((n_tp, nx)), DMA((n_tp, nx)),
                 DMA((2, n_tp, nx)), DMA((2, n_tp, nx)),
+                pltpu.SMEM((n_seq,), jnp.int32),
             ],
             compiler_params=pltpu.CompilerParams(
                 collective_id=0, has_side_effects=True, vmem_limit_bytes=46 * MIB),
             name='main',
-        )(positions, in_hbm(hidden), in_hbm(norm_scale.reshape(d_model // 128, 128)),
+        )(in_hbm(positions), in_hbm(hidden), in_hbm(norm_scale.reshape(d_model // 128, 128)),
           in_hbm(positions.reshape(1, n_seq)), in_hbm(w_qkv), in_hbm(k_cache.reshape(flat)),
           in_hbm(v_cache.reshape(flat)), in_hbm(w_out))
 

time: 55.8 us -> 55.8 us (level)
  no operation moved by 1% of the time
where the time goes in v7:
time: 55.8 us; the launch traced here: 55.7 us
  Pallas kernels  55.1 us (99%)
  between operations  0.66 us (1%)
    pallas_call x1, Pallas kernels, local_step(): pl.pallas_call(functools.partial(main_kernel, (q_per_kv, head, pitch, n_t...  50.6 us
    pallas_call x1, Pallas kernels, local_step(): pl.pallas_call(functools.partial(write_kernel, (q_per_kv, head, pitch, n_...  4.46 us

profile of v7, /device:TPU:97, one launch (start us, length us, event | category | flops | bytes accessed | tf_op | source)
XLA Modules:
  0.0 55.7 jit_solution(15998013819842001884)
XLA Ops:
  0.6 0.0 copy-start
  0.6 50.6 %main.1 = (f32[2,720,128]{2,1,0:T(8,128)S(1)}, bf16[64,256,128]{2,1,0:T(8,128)(2,1)S(1)}, bf16[64,256,128]{2,1,0:T(8,128)(2,1)S(1)}, f32[64,8192]{1,0:T(8,128)S(1)}) custom-call(s32[64]{0:T(128)} %pos_ref.1, bf16[64,8192]{1,0:T(8,128)(2,1)} %h_hbm.1, bf16[64,128]{1,0:T(8,128)(2,1)} %bitcast.9, s32[1,64]{1,0:T(1,128)} %bitcast.6, bf16[8192,2560]{1,0:T(8,128)(2,1)} %w_ref.1, ...), custom_call_target="tpu_custom_call" | custom-call | tf_op jit(solution)/shard_map/main/pallas_call | solution.py:415
  51.3 0.0 copy-done
  51.3 4.5 %write.1 = (bf16[64,8192]{1,0:T(8,128)(2,1)}, bf16[64,256,128]{2,1,0:T(8,128)(2,1)}, bf16[64,256,128]{2,1,0:T(8,128)(2,1)}, bf16[64,256,128]{2,1,0:T(8,128)(2,1)S(1)}, bf16[64,256,128]{2,1,0:T(8,128)(2,1)S(1)}) custom-call(s32[64]{0:T(128)S(1)} %copy-done, ...), custom_call_target="tpu_custom_call", output_to_operand_aliasing={{3}: (3, {}), {4}: (4, {})} | custom-call | tf_op jit(solution)/shard_map/write/pallas_call | solution.py:452
Async XLA Ops:
  0.6 50.6 %copy-start = (s32[64]{0:T(128)S(1)}, s32[64]{0:T(128)}, u32[]{:S(2)}) copy-start(s32[64]{0:T(128)} %pos_ref.1) | copy-start | bytes 772

commit v8 on v7

--- a/solution.py
+++ b/solution.py
@@ -35,8 +35,8 @@
 
 
 def main_kernel(dims, pos_flat, h_hbm, scale_hbm, pos_hbm, w_ref, k_hbm, v_hbm, wo_ref, out_ref, kbuf, vbuf, res_ref,
-                h_ref, scale_ref, pos_ref, wbuf, u_ref, acc, gain, o_ref, rbuf, abuf, attn, lhs, wobuf, pbuf, ybuf, hbuf,
-                hsem, wsem, csem, s_part, r_part, wosem, hosem, rs_s, rs_r, ab_s, ab_r, y_s, y_r, a_s, a_r, b_s, b_r,
+                h_ref, scale_ref, pos_ref, wbuf, u_ref, acc, gain, o_ref, cbuf, mix, rbuf, abuf, attn, lhs, wobuf, pbuf, ybuf, hbuf,
+                hsem, wsem, csem, s_part, r_part, wosem, hosem, c_s, c_r, rs_s, rs_r, ab_s, ab_r, y_s, y_r, a_s, a_r, b_s, b_r,
                 d_s, d_r, pos_smem):
     n_seq, d_model = h_ref.shape
     q_per_kv, head, pitch, n_tp, n_sp = dims
@@ -72,21 +72,19 @@
             wo_ref.at[:, ds((core * n_tp + yat(j)) * cols, cols, cols)], wobuf.at[j], wosem.at[j])
 
     def chunk_of(d):
-        return lax.rem(s + d, n_sp)
+        return lax.rem(x + d // CORES, nx) * CORES + (core if d % CORES == 0 else 1 - core)
 
     def ccopy(d, which):
         src, dst = ((k_hbm, kbuf), (v_hbm, vbuf))[which]
         cut = pl.ds(chunk_of(d) * per, per)
         return pltpu.make_async_copy(src.at[cut], dst.at[cut], csem.at[which, d])
-
-    def owner(t):
-        return 1 + (t + n_sp // 2 - 2) % (n_sp - 1)
 
     hcopy = pltpu.make_async_copy(
         h_hbm.at[ds(x * seqs, seqs, seqs), ds((core * n_tp + y) * cols, cols, cols)], hbuf, hosem)
     far_tp = sorted(range(1, n_tp), key=lambda d: -min(d, n_tp - d))
     far_x = sorted(range(1, nx), key=lambda d: -min(d, nx - d))
     order = far_tp + [0]
+    chips = far_x + [0]
     loads = [
         pltpu.make_async_copy(src, dst, hsem.at[i])
         for i, (src, dst) in enumerate(
@@ -97,8 +95,9 @@
     for i in range(n_blk):
         wload(i).start()
     barrier = pltpu.get_barrier_semaphore()
-    for d in range(1, n_sp):
-        pl.semaphore_signal(barrier, inc=1, device_id={'sp': lax.rem(s + d, n_sp)}, device_id_type=MESH)
+    pl.semaphore_signal(barrier, inc=1, device_id={'sp': partner}, device_id_type=MESH)
+    for d in range(1, nx):
+        pl.semaphore_signal(barrier, inc=1, device_id={'sp': xat(d)}, device_id_type=MESH)
     for d in range(1, n_tp):
         pl.semaphore_signal(barrier, inc=1, device_id={'tp': yat(d)}, device_id_type=MESH)
     for load in loads:
@@ -149,7 +148,7 @@
 
         @pl.when(i == CACHE_STEP)
         def _():
-            for d in [owner(t) for t in range(n_sp - 1)] + [0]:
+            for d in [CORES * e + p for e in chips for p in (1, 0)]:
                 ccopy(d, 0).start()
                 ccopy(d, 1).start()
 
@@ -157,7 +156,7 @@
         return carry
 
     lax.fori_loop(0, n_blk, mm, 0)
-    pl.semaphore_wait(barrier, n_sp + n_tp - 2)
+    pl.semaphore_wait(barrier, nx + n_tp - 1)
     for j in order:
         wcopy(j).start()
     hcopy.start()
@@ -176,9 +175,34 @@
     for j in range(q_per_kv + 2):
         psend(j).wait_recv()
 
-    def rs(d):
-        to = chunk_of(d)
-        return rcopy(o_ref.at[d], rbuf.at[d], rs_s.at[d], rs_r.at[d], sp=to)
+    def give(e):
+        return rcopy(o_ref.at[CORES * e + 1], cbuf.at[e], c_s.at[e], c_r.at[e], sp=partner)
+
+    def rs(e):
+        return rcopy(mix.at[e], rbuf.at[e], rs_s.at[e], rs_r.at[e], sp=xat(e))
+
+    def merge(parts):
+        tops = [p[n_rows:n_rows + 1, :] for p in parts]
+        sums = [p[n_rows + 1:n_rows + 2, :] for p in parts]
+        top = functools.reduce(jnp.maximum, tops)
+        facs = [jnp.exp(t - top) for t in tops]
+        tot = functools.reduce(jnp.add, [f * l for f, l in zip(facs, sums)])
+        return top, tot, facs
+
+    def weigh(parts, facs):
+        pad = jnp.zeros((n_rows - len(facs), n_rows), F32)
+        fac = jnp.transpose(jnp.concatenate(facs + [pad], axis=0))
+        return functools.reduce(
+            jnp.add, [p[0:n_rows, :] * fac[:, j:j + 1] for j, p in enumerate(parts)])
+
+    def pair(e):
+        give(e).wait_recv()
+        parts = [o_ref.at[CORES * e], cbuf.at[e]]
+        top, tot, facs = merge(parts)
+        mix[e, 0:n_rows, :] = weigh(parts, facs)
+        mix[e, n_rows:n_rows + 8, :] = jnp.concatenate([top, tot, jnp.zeros((6, n_rows), F32)], axis=0)
+        if e:
+            rs(e).start()
 
     def attend(d):
         i = chunk_of(d)
@@ -218,29 +242,21 @@
         pad = jnp.zeros((6, n_rows), F32)
         o_ref[d, n_rows:n_rows + 8, :] = jnp.concatenate([top_row, tot_row, pad], axis=0)
 
-    def sweep(t, carry):
-        d = owner(t)
-        attend(d)
-        rs(d).start()
-        return carry
-
-    lax.fori_loop(0, n_sp - 1, sweep, 0)
-    attend(0)
-    parts = [o_ref.at[0]]
-    for d in range(1, n_sp):
-        rs(d).wait_recv()
-        parts.append(rbuf.at[d])
-    tops = [p[n_rows:n_rows + 1, :] for p in parts]
-    sums = [p[n_rows + 1:n_rows + 2, :] for p in parts]
-    top = functools.reduce(jnp.maximum, tops)
-    facs = [jnp.exp(t - top) for t in tops]
-    tot = functools.reduce(jnp.add, [f * l for f, l in zip(facs, sums)])
-    fac = jnp.concatenate([f / tot for f in facs], axis=0)
-    pad = jnp.zeros((n_rows - n_sp, n_rows), F32)
-    fac = jnp.transpose(jnp.concatenate([fac, pad], axis=0))
-    val = parts[0][0:n_rows, :] * fac[:, 0:1]
-    for j in range(1, n_sp):
-        val = val + parts[j][0:n_rows, :] * fac[:, j:j + 1]
+    last = None
+    for e in chips:
+        attend(CORES * e + 1)
+        give(e).start()
+        attend(CORES * e)
+        if last is not None:
+            pair(last)
+        last = e
+    pair(last)
+    parts = [mix.at[0]]
+    for e in reversed(far_x):
+        rs(e).wait_recv()
+        parts.append(rbuf.at[e])
+    _, tot, facs = merge(parts)
+    val = weigh(parts, [f / tot for f in facs])
     attn[0] = val
 
     swap = rcopy(attn.at[0], abuf.at[core], ab_s, ab_r, sp=partner)
@@ -294,9 +310,9 @@
         cp.start()
         sends.append(cp)
 
-    for e in far_tp:
+    for e in reversed(far_tp):
         go(0, 0, 0, (a_s, a_r), {'tp': yat(e)}, e, 0)
-    for e in far_x:
+    for e in reversed(far_x):
         go(0, 0, 1, (b_s, b_r), {'sp': xat(e)}, 0, e)
     fwd(0, 0, 0)
     fwd(0, 0, 1)
@@ -326,8 +342,10 @@
                 rcopy(ref, ref, d_s.at[part, dy, dx], d_r.at[part, dy, dx], sp=partner).wait_recv()
     for cp in sends:
         cp.wait_send()
-    for d in range(1, n_sp):
-        rs(d).wait_send()
+    for e in range(1, nx):
+        rs(e).wait_send()
+    for e in range(nx):
+        give(e).wait_send()
     for d in range(1, n_tp):
         ysend(d).wait_send()
     for j in range(q_per_kv + 2):
@@ -427,7 +445,9 @@
                 pltpu.VMEM((n_seq, grp_cols), F32),
                 pltpu.VMEM((d_model // 128, 128), F32),
                 pltpu.VMEM((n_sp, n_rows + 8, head), F32),
-                pltpu.VMEM((n_sp, n_rows + 8, head), F32),
+                pltpu.VMEM((nx, n_rows + 8, head), F32),
+                pltpu.VMEM((nx, n_rows + 8, head), F32),
+                pltpu.VMEM((nx, n_rows + 8, head), F32),
                 pltpu.VMEM((CORES, n_rows, head), F32),
                 pltpu.VMEM((1, n_rows, head), F32),
                 pltpu.VMEM((CORES * per, depth), BF16),
@@ -437,7 +457,7 @@
                 pltpu.VMEM((CORES * per, cols), BF16),
                 DMA((4,)), DMA((n_blk,)), DMA((2, n_sp)), DMA((q_per_kv + 2,)), DMA((q_per_kv + 2,)),
                 DMA((n_tp,)), DMA,
-                DMA((n_sp,)), DMA((n_sp,)), DMA, DMA, DMA((n_tp,)), DMA((n_tp,)),
+                DMA((nx,)), DMA((nx,)), DMA((nx,)), DMA((nx,)), DMA, DMA, DMA((n_tp,)), DMA((n_tp,)),
                 DMA((n_tp, nx)), DMA((n_tp, nx)), DMA((n_tp, nx)), DMA((n_tp, nx)),
                 DMA((2, n_tp, nx)), DMA((2, n_tp, nx)),
                 pltpu.SMEM((n_seq,), jnp.int32),

time: 55.8 us -> 55.6 us (level)
  no operation moved by 1% of the time
where the time goes in v8:
time: 55.6 us; the launch traced here: 55.5 us
  Pallas kernels  54.9 us (99%)
  between operations  0.66 us (1%)
    pallas_call x1, Pallas kernels, local_step(): pl.pallas_call(functools.partial(main_kernel, (q_per_kv, head, pitch, n_t...  50.4 us
    pallas_call x1, Pallas kernels, local_step(): pl.pallas_call(functools.partial(write_kernel, (q_per_kv, head, pitch, n_...  4.46 us

profile of v8, /device:TPU:97, one launch (start us, length us, event | category | flops | bytes accessed | tf_op | source)
XLA Modules:
  0.0 55.5 jit_solution(1763805632262231333)
XLA Ops:
  0.6 0.0 copy-start
  0.6 50.4 %main.1 = (f32[2,720,128]{2,1,0:T(8,128)S(1)}, bf16[64,256,128]{2,1,0:T(8,128)(2,1)S(1)}, bf16[64,256,128]{2,1,0:T(8,128)(2,1)S(1)}, f32[64,8192]{1,0:T(8,128)S(1)}) custom-call(s32[64]{0:T(128)} %pos_ref.1, bf16[64,8192]{1,0:T(8,128)(2,1)} %h_hbm.1, bf16[64,128]{1,0:T(8,128)(2,1)} %bitcast.9, s32[1,64]{1,0:T(1,128)} %bitcast.6, bf16[8192,2560]{1,0:T(8,128)(2,1)} %w_ref.1, ...), custom_call_target="tpu_custom_call" | custom-call | tf_op jit(solution)/shard_map/main/pallas_call | solution.py:433
  51.1 0.0 copy-done
  51.1 4.5 %write.1 = (bf16[64,8192]{1,0:T(8,128)(2,1)}, bf16[64,256,128]{2,1,0:T(8,128)(2,1)}, bf16[64,256,128]{2,1,0:T(8,128)(2,1)}, bf16[64,256,128]{2,1,0:T(8,128)(2,1)S(1)}, bf16[64,256,128]{2,1,0:T(8,128)(2,1)S(1)}) custom-call(s32[64]{0:T(128)S(1)} %copy-done, ...), custom_call_target="tpu_custom_call", output_to_operand_aliasing={{3}: (3, {}), {4}: (4, {})} | custom-call | tf_op jit(solution)/shard_map/write/pallas_call | solution.py:472
Async XLA Ops:
  0.6 50.4 %copy-start = (s32[64]{0:T(128)S(1)}, s32[64]{0:T(128)}, u32[]{:S(2)}) copy-start(s32[64]{0:T(128)} %pos_ref.1) | copy-start | bytes 772

commit v9 on v8

--- a/solution.py
+++ b/solution.py
@@ -15,6 +15,7 @@
 VMEM = pl.BlockSpec(memory_space=pltpu.VMEM)
 SMEM = pl.BlockSpec(memory_space=pltpu.SMEM)
 CORES = 2
+RING_HEADS = 1
 CACHE_STEP = 10
 MIB = 1024 * 1024
 
@@ -35,12 +36,15 @@
 
 
 def main_kernel(dims, pos_flat, h_hbm, scale_hbm, pos_hbm, w_ref, k_hbm, v_hbm, wo_ref, out_ref, kbuf, vbuf, res_ref,
-                h_ref, scale_ref, pos_ref, wbuf, u_ref, acc, gain, o_ref, cbuf, mix, rbuf, abuf, attn, lhs, wobuf, pbuf, ybuf, hbuf,
+                h_ref, scale_ref, pos_ref, wbuf, u_ref, acc, gain, wring, o_ref, cbuf, mix, rbuf, abuf, attn, lhs, wobuf, pbuf, ybuf, hbuf,
                 hsem, wsem, csem, s_part, r_part, wosem, hosem, c_s, c_r, rs_s, rs_r, ab_s, ab_r, y_s, y_r, a_s, a_r, b_s, b_r,
-                d_s, d_r, pos_smem):
+                d_s, d_r, pos_smem, rsem, s_ring, r_ring):
     n_seq, d_model = h_ref.shape
     q_per_kv, head, pitch, n_tp, n_sp = dims
-    n_blk, blk, grp = wbuf.shape
+    n_blk, blk, lcols = wbuf.shape
+    n_rblk, rblk, rcols = wring.shape
+    rh = rcols // head
+    grp = (q_per_kv + 2) * head
     groups = out_ref.shape[0]
     heads = groups * q_per_kv
     rows2 = kbuf.shape[1]
@@ -65,7 +69,11 @@
 
     def wload(i):
         return pltpu.make_async_copy(
-            w_ref.at[ds(i * blk, blk, blk), ds(core * grp, grp, 128)], wbuf.at[i], wsem.at[i])
+            w_ref.at[ds(i * blk, blk, blk), ds(core * grp + nx * rcols, lcols, 128)], wbuf.at[i], wsem.at[i])
+
+    def rload(i):
+        return pltpu.make_async_copy(
+            w_ref.at[pl.ds(i * rblk, rblk), ds(core * grp + x * rcols, rcols, 128)], wring.at[i], rsem.at[i])
 
     def wcopy(j):
         return pltpu.make_async_copy(
@@ -92,6 +100,8 @@
     ]
     for load in loads:
         load.start()
+    for i in range(n_rblk):
+        rload(i).start()
     for i in range(n_blk):
         wload(i).start()
     barrier = pltpu.get_barrier_semaphore()
@@ -137,9 +147,35 @@
     cos_t = jnp.cos(angle)
     sin_t = jnp.where(lane < half, -jnp.sin(angle), jnp.sin(angle))
 
-    def psend(j):
-        ref = out_ref.at[core, pl.ds(j * pitch, n_seq)]
-        return rcopy(ref, ref, s_part.at[j], r_part.at[j], sp=partner)
+    def finish(val, rotate):
+        val = jnp.clip(val.astype(BF16), -8.0, 8.0).astype(F32)
+        if rotate:
+            val = (val * cos_t + pltpu.roll(val, half, 1) * sin_t).astype(BF16).astype(F32)
+        return val
+
+    def slab(cx):
+        return out_ref.at[core, ds(cx * rh * pitch, (rh - 1) * pitch + n_seq, 8)]
+
+    def rsend(e):
+        return rcopy(slab(x), slab(x), s_ring.at[e], r_ring.at[e], sp=xat(e))
+
+    n_local = lcols // head
+
+    def psend(d):
+        ref = slab(lax.rem(x + nx - d, nx)) if d < nx else out_ref.at[core, pl.ds((nx * rh + d - nx) * pitch, n_seq)]
+        return rcopy(ref, ref, s_part.at[d], r_part.at[d], sp=partner)
+
+    tot = None
+    for i in range(n_rblk):
+        rload(i).wait()
+        prod = jnp.dot(u_ref[:, i * rblk:(i + 1) * rblk], wring[i], preferred_element_type=F32)
+        tot = prod if tot is None else tot + prod
+    for t in range(rh):
+        out_ref[core, ds((x * rh + t) * pitch, n_seq, 8), :] = finish(tot[:, t * head:(t + 1) * head], True)
+    pl.semaphore_wait(barrier, nx + n_tp - 1)
+    for e in far_x:
+        rsend(e).start()
+    psend(0).start()
 
     acc[...] = jnp.zeros_like(acc)
 
@@ -156,24 +192,26 @@
         return carry
 
     lax.fori_loop(0, n_blk, mm, 0)
-    pl.semaphore_wait(barrier, nx + n_tp - 1)
     for j in order:
         wcopy(j).start()
     hcopy.start()
-    for j in range(q_per_kv + 2):
-        val = jnp.clip(acc[:, j * head:(j + 1) * head].astype(BF16), -8.0, 8.0).astype(F32)
-        if j < q_per_kv + 1:
-            val = (val * cos_t + pltpu.roll(val, half, 1) * sin_t).astype(BF16).astype(F32)
-        out_ref[core, j * pitch:j * pitch + n_seq, :] = val
-        if j > 0:
-            psend(j - 1).start()
-    psend(q_per_kv + 1).start()
+    for t in range(n_local):
+        at = nx * rh + t
+        out_ref[core, at * pitch:at * pitch + n_seq, :] = finish(
+            acc[:, t * head:(t + 1) * head], at < q_per_kv + 1)
+        if t > 0:
+            psend(nx + t - 1).start()
+    psend(nx + n_local - 1).start()
+    for e in reversed(far_x):
+        rsend(e).wait_recv()
+        psend(e).start()
+
     colj = lax.broadcasted_iota(jnp.int32, (heads, rows2), 1)
     rown = lax.broadcasted_iota(jnp.int32, (heads, rows2), 0)
     same = lax.rem(colj, groups) == rown // q_per_kv
     eye = lax.broadcasted_iota(jnp.int32, (n_rows, n_rows), 0) == lax.broadcasted_iota(jnp.int32, (n_rows, n_rows), 1)
-    for j in range(q_per_kv + 2):
-        psend(j).wait_recv()
+    for d in range(nx + n_local):
+        psend(d).wait_recv()
 
     def give(e):
         return rcopy(o_ref.at[CORES * e + 1], cbuf.at[e], c_s.at[e], c_r.at[e], sp=partner)
@@ -348,8 +386,10 @@
         give(e).wait_send()
     for d in range(1, n_tp):
         ysend(d).wait_send()
-    for j in range(q_per_kv + 2):
-        psend(j).wait_send()
+    for d in range(nx + n_local):
+        psend(d).wait_send()
+    for e in range(1, nx):
+        rsend(e).wait_send()
 
 
 def write_kernel(dims, pos_ref, qkv_ref, res_ref, k_ref, v_ref, h_out, ko_ref, vo_ref, kbuf, vbuf, hbuf, osem, hsem):
@@ -419,7 +459,9 @@
         q_per_kv = w_qkv.shape[1] // (kv_local * head) - 2
         heads = kv_local * q_per_kv
         grp_cols = (q_per_kv + 2) * head
-        n_blk = 16
+        n_blk, n_rblk = 16, 2
+        ring_cols = RING_HEADS * head
+        local_cols = grp_cols - (n_sp // CORES) * ring_cols
         pitch = n_seq + 8
         per = n_seq // n_sp
         n_rows = per * heads
@@ -440,10 +482,11 @@
                 pltpu.VMEM(hidden.shape, BF16),
                 pltpu.VMEM((d_model // 128, 128), BF16),
                 pltpu.VMEM((1, n_seq), jnp.int32),
-                pltpu.VMEM((n_blk, d_model // n_blk, grp_cols), BF16),
+                pltpu.VMEM((n_blk, d_model // n_blk, local_cols), BF16),
                 pltpu.VMEM((n_seq, d_model), BF16),
-                pltpu.VMEM((n_seq, grp_cols), F32),
+                pltpu.VMEM((n_seq, local_cols), F32),
                 pltpu.VMEM((d_model // 128, 128), F32),
+                pltpu.VMEM((n_rblk, d_model // n_rblk, ring_cols), BF16),
                 pltpu.VMEM((n_sp, n_rows + 8, head), F32),
                 pltpu.VMEM((nx, n_rows + 8, head), F32),
                 pltpu.VMEM((nx, n_rows + 8, head), F32),
@@ -461,6 +504,7 @@
                 DMA((n_tp, nx)), DMA((n_tp, nx)), DMA((n_tp, nx)), DMA((n_tp, nx)),
                 DMA((2, n_tp, nx)), DMA((2, n_tp, nx)),
                 pltpu.SMEM((n_seq,), jnp.int32),
+                DMA((n_rblk,)), DMA((nx,)), DMA((nx,)),
             ],
             compiler_params=pltpu.CompilerParams(
                 collective_id=0, has_side_effects=True, vmem_limit_bytes=46 * MIB),

time: 55.6 us -> 53.1 us (0.955)
  Pallas kernels: 54.9 us -> 52.4 us
    pallas_call x1, Pallas kernels: 50.4 us -> 47.9 us  [local_step(): pl.pallas_call(functools.partial(main_kernel, (q_per_kv, head, pitch, n_t...]
where the time goes in v9:
time: 53.1 us
  Pallas kernels  52.4 us (99%)
  between operations  0.66 us (1%)
    pallas_call x1, Pallas kernels, local_step(): pl.pallas_call(functools.partial(main_kernel, (q_per_kv, head, pitch, n_t...  47.9 us
    pallas_call x1, Pallas kernels, local_step(): pl.pallas_call(functools.partial(write_kernel, (q_per_kv, head, pitch, n_...  4.46 us

profile of v9, /device:TPU:97, one launch (start us, length us, event | category | flops | bytes accessed | tf_op | source)
XLA Modules:
  0.0 53.1 jit_solution(18250039461512919351)
XLA Ops:
  0.6 0.0 copy-start
  0.6 47.9 %main.1 = (f32[2,720,128]{2,1,0:T(8,128)S(1)}, bf16[64,256,128]{2,1,0:T(8,128)(2,1)S(1)}, bf16[64,256,128]{2,1,0:T(8,128)(2,1)S(1)}, f32[64,8192]{1,0:T(8,128)S(1)}) custom-call(s32[64]{0:T(128)} %pos_ref.1, bf16[64,8192]{1,0:T(8,128)(2,1)} %h_hbm.1, bf16[64,128]{1,0:T(8,128)(2,1)} %bitcast.9, s32[1,64]{1,0:T(1,128)} %bitcast.6, bf16[8192,2560]{1,0:T(8,128)(2,1)} %w_ref.1, ...), custom_call_target="tpu_custom_call" | custom-call | tf_op jit(solution)/shard_map/main/pallas_call | solution.py:475
  48.6 0.0 copy-done
  48.6 4.5 %write.1 = (bf16[64,8192]{1,0:T(8,128)(2,1)}, bf16[64,256,128]{2,1,0:T(8,128)(2,1)}, bf16[64,256,128]{2,1,0:T(8,128)(2,1)}, bf16[64,256,128]{2,1,0:T(8,128)(2,1)S(1)}, bf16[64,256,128]{2,1,0:T(8,128)(2,1)S(1)}) custom-call(s32[64]{0:T(128)S(1)} %copy-done, ...), custom_call_target="tpu_custom_call", output_to_operand_aliasing={{3}: (3, {}), {4}: (4, {})} | custom-call | tf_op jit(solution)/shard_map/write/pallas_call | solution.py:516
Async XLA Ops:
  0.6 48.0 %copy-start = (s32[64]{0:T(128)S(1)}, s32[64]{0:T(128)}, u32[]{:S(2)}) copy-start(s32[64]{0:T(128)} %pos_ref.1) | copy-start | bytes 772

commit v10 on v9

--- a/solution.py
+++ b/solution.py
@@ -16,7 +16,8 @@
 SMEM = pl.BlockSpec(memory_space=pltpu.SMEM)
 CORES = 2
 RING_HEADS = 1
-CACHE_STEP = 10
+CACHE_STEP = 12
+WINDOW = 5
 MIB = 1024 * 1024
 
 
@@ -87,6 +88,11 @@
         cut = pl.ds(chunk_of(d) * per, per)
         return pltpu.make_async_copy(src.at[cut], dst.at[cut], csem.at[which, d])
 
+    def cache_load(e):
+        for p in (1, 0):
+            ccopy(CORES * e + p, 0).start()
+            ccopy(CORES * e + p, 1).start()
+
     hcopy = pltpu.make_async_copy(
         h_hbm.at[ds(x * seqs, seqs, seqs), ds((core * n_tp + y) * cols, cols, cols)], hbuf, hosem)
     far_tp = sorted(range(1, n_tp), key=lambda d: -min(d, n_tp - d))
@@ -102,8 +108,6 @@
         load.start()
     for i in range(n_rblk):
         rload(i).start()
-    for i in range(n_blk):
-        wload(i).start()
     barrier = pltpu.get_barrier_semaphore()
     pl.semaphore_signal(barrier, inc=1, device_id={'sp': partner}, device_id_type=MESH)
     for d in range(1, nx):
@@ -112,6 +116,8 @@
         pl.semaphore_signal(barrier, inc=1, device_id={'tp': yat(d)}, device_id_type=MESH)
     for load in loads:
         load.wait()
+    for i in range(WINDOW):
+        wload(i).start()
 
     lanes = 128
     zero = jnp.zeros((n_seq, lanes), F32)
@@ -182,18 +188,20 @@
     def mm(i, carry):
         wload(i).wait()
 
+        @pl.when(i + WINDOW < n_blk)
+        def _():
+            wload(i + WINDOW).start()
+
         @pl.when(i == CACHE_STEP)
         def _():
-            for d in [CORES * e + p for e in chips for p in (1, 0)]:
-                ccopy(d, 0).start()
-                ccopy(d, 1).start()
+            cache_load(chips[0])
 
         acc[...] += jnp.dot(u_ref[:, ds(i * blk, blk, blk)], wbuf[i], preferred_element_type=F32)
         return carry
 
     lax.fori_loop(0, n_blk, mm, 0)
-    for j in order:
-        wcopy(j).start()
+    for e in chips[1:]:
+        cache_load(e)
     hcopy.start()
     for t in range(n_local):
         at = nx * rh + t
@@ -281,13 +289,18 @@
         o_ref[d, n_rows:n_rows + 8, :] = jnp.concatenate([top_row, tot_row, pad], axis=0)
 
     last = None
-    for e in chips:
+    for t, e in enumerate(chips):
+        if t == nx // 2:
+            for j in order[:n_tp // 2]:
+                wcopy(j).start()
         attend(CORES * e + 1)
         give(e).start()
         attend(CORES * e)
         if last is not None:
             pair(last)
         last = e
+    for j in order[n_tp // 2:]:
+        wcopy(j).start()
     pair(last)
     parts = [mix.at[0]]
     for e in reversed(far_x):

time: 53.1 us -> 49.5 us (0.932)
  Pallas kernels: 52.4 us -> 48.7 us
    pallas_call x1, Pallas kernels: 47.9 us -> 44.3 us  [local_step(): pl.pallas_call(functools.partial(main_kernel, (q_per_kv, head, pitch, n_t...]
where the time goes in v10:
time: 49.5 us; the launch traced here: 49.4 us
  Pallas kernels  48.7 us (98%)
  between operations  0.66 us (1%)
    pallas_call x1, Pallas kernels, local_step(): pl.pallas_call(functools.partial(main_kernel, (q_per_kv, head, pitch, n_t...  44.3 us
    pallas_call x1, Pallas kernels, local_step(): pl.pallas_call(functools.partial(write_kernel, (q_per_kv, head, pitch, n_...  4.46 us

profile of v10, /device:TPU:97, one launch (start us, length us, event | category | flops | bytes accessed | tf_op | source)
XLA Modules:
  0.0 49.4 jit_solution(4207008628703977847)
XLA Ops:
  0.6 0.0 copy-start
  0.6 44.3 %main.1 = (f32[2,720,128]{2,1,0:T(8,128)S(1)}, bf16[64,256,128]{2,1,0:T(8,128)(2,1)S(1)}, bf16[64,256,128]{2,1,0:T(8,128)(2,1)S(1)}, f32[64,8192]{1,0:T(8,128)S(1)}) custom-call(s32[64]{0:T(128)} %pos_ref.1, bf16[64,8192]{1,0:T(8,128)(2,1)} %h_hbm.1, bf16[64,128]{1,0:T(8,128)(2,1)} %bitcast.9, s32[1,64]{1,0:T(1,128)} %bitcast.6, bf16[8192,2560]{1,0:T(8,128)(2,1)} %w_ref.1, ...), custom_call_target="tpu_custom_call" | custom-call | tf_op jit(solution)/shard_map/main/pallas_call | solution.py:488
  44.9 0.0 copy-done
  44.9 4.5 %write.1 = (bf16[64,8192]{1,0:T(8,128)(2,1)}, bf16[64,256,128]{2,1,0:T(8,128)(2,1)}, bf16[64,256,128]{2,1,0:T(8,128)(2,1)}, bf16[64,256,128]{2,1,0:T(8,128)(2,1)S(1)}, bf16[64,256,128]{2,1,0:T(8,128)(2,1)S(1)}) custom-call(s32[64]{0:T(128)S(1)} %copy-done, ...), custom_call_target="tpu_custom_call", output_to_operand_aliasing={{3}: (3, {}), {4}: (4, {})} | custom-call | tf_op jit(solution)/shard_map/write/pallas_call | solution.py:529
Async XLA Ops:
  0.6 44.3 %copy-start = (s32[64]{0:T(128)S(1)}, s32[64]{0:T(128)}, u32[]{:S(2)}) copy-start(s32[64]{0:T(128)} %pos_ref.1) | copy-start | bytes 772

commit v11 on v10

--- a/solution.py
+++ b/solution.py
@@ -18,6 +18,8 @@
 RING_HEADS = 1
 CACHE_STEP = 12
 WINDOW = 5
+H_PARTS = 4
+WO_PARTS = 2
 MIB = 1024 * 1024
 
 
@@ -76,9 +78,17 @@
         return pltpu.make_async_copy(
             w_ref.at[pl.ds(i * rblk, rblk), ds(core * grp + x * rcols, rcols, 128)], wring.at[i], rsem.at[i])
 
-    def wcopy(j):
+    def wcopy(j, part):
+        rows = wobuf.shape[1] // WO_PARTS
+        cut = pl.ds(part * rows, rows)
         return pltpu.make_async_copy(
-            wo_ref.at[:, ds((core * n_tp + yat(j)) * cols, cols, cols)], wobuf.at[j], wosem.at[j])
+            wo_ref.at[cut, ds((core * n_tp + yat(j)) * cols, cols, cols)], wobuf.at[j, cut], wosem.at[j, part])
+
+    def out_load(n):
+        for _ in range(min(n, len(todo))):
+            j = todo.pop(0)
+            for part in range(WO_PARTS):
+                wcopy(j, part).start()
 
     def chunk_of(d):
         return lax.rem(x + d // CORES, nx) * CORES + (core if d % CORES == 0 else 1 - core)
@@ -99,10 +109,13 @@
     far_x = sorted(range(1, nx), key=lambda d: -min(d, nx - d))
     order = far_tp + [0]
     chips = far_x + [0]
+    todo = list(order)
+    cuts = [pl.ds(i * (d_model // H_PARTS), d_model // H_PARTS) for i in range(H_PARTS)]
     loads = [
         pltpu.make_async_copy(src, dst, hsem.at[i])
         for i, (src, dst) in enumerate(
-            ((h_hbm, h_ref), (scale_hbm, scale_ref), (pos_hbm, pos_ref), (pos_flat, pos_smem)))
+            [(h_hbm.at[:, cut], h_ref.at[:, cut]) for cut in cuts]
+            + [(scale_hbm, scale_ref), (pos_hbm, pos_ref), (pos_flat, pos_smem)])
     ]
     for load in loads:
         load.start()
@@ -290,22 +303,21 @@
 
     last = None
     for t, e in enumerate(chips):
-        if t == nx // 2:
-            for j in order[:n_tp // 2]:
-                wcopy(j).start()
+        if t >= nx // 2:
+            out_load(1)
         attend(CORES * e + 1)
         give(e).start()
         attend(CORES * e)
         if last is not None:
             pair(last)
         last = e
-    for j in order[n_tp // 2:]:
-        wcopy(j).start()
+    out_load(1)
     pair(last)
     parts = [mix.at[0]]
     for e in reversed(far_x):
         rs(e).wait_recv()
         parts.append(rbuf.at[e])
+    out_load(len(todo))
     _, tot, facs = merge(parts)
     val = weigh(parts, [f / tot for f in facs])
     attn[0] = val
@@ -322,7 +334,8 @@
         return rcopy(pbuf.at[d], ybuf.at[d], y_s.at[d], y_r.at[d], tp=yat(d))
 
     def proj(j):
-        wcopy(j).wait()
+        for part in range(WO_PARTS):
+            wcopy(j, part).wait()
         pbuf[j] = jnp.dot(lhs[...], wobuf[j], preferred_element_type=F32)
 
     for j in order:
@@ -511,8 +524,8 @@
                 pltpu.VMEM((n_tp, CORES * per, cols), F32),
                 pltpu.VMEM((n_tp, CORES * per, cols), F32),
                 pltpu.VMEM((CORES * per, cols), BF16),
-                DMA((4,)), DMA((n_blk,)), DMA((2, n_sp)), DMA((q_per_kv + 2,)), DMA((q_per_kv + 2,)),
-                DMA((n_tp,)), DMA,
+                DMA((H_PARTS + 3,)), DMA((n_blk,)), DMA((2, n_sp)), DMA((q_per_kv + 2,)), DMA((q_per_kv + 2,)),
+                DMA((n_tp, WO_PARTS)), DMA,
                 DMA((nx,)), DMA((nx,)), DMA((nx,)), DMA((nx,)), DMA, DMA, DMA((n_tp,)), DMA((n_tp,)),
                 DMA((n_tp, nx)), DMA((n_tp, nx)), DMA((n_tp, nx)), DMA((n_tp, nx)),
                 DMA((2, n_tp, nx)), DMA((2, n_tp, nx)),

time: 49.5 us -> 49.5 us (level)
  no operation moved by 1% of the time
where the time goes in v11:
time: 49.5 us; the launch traced here: 49.4 us
  Pallas kernels  48.8 us (99%)
  between operations  0.66 us (1%)
    pallas_call x1, Pallas kernels, local_step(): pl.pallas_call(functools.partial(main_kernel, (q_per_kv, head, pitch, n_t...  44.3 us
    pallas_call x1, Pallas kernels, local_step(): pl.pallas_call(functools.partial(write_kernel, (q_per_kv, head, pitch, n_...  4.46 us

profile of v11, /device:TPU:97, one launch (start us, length us, event | category | flops | bytes accessed | tf_op | source)
XLA Modules:
  0.0 49.4 jit_solution(2681918918753941451)
XLA Ops:
  0.6 0.0 copy-start
  0.6 44.3 %main.1 = (f32[2,720,128]{2,1,0:T(8,128)S(1)}, bf16[64,256,128]{2,1,0:T(8,128)(2,1)S(1)}, bf16[64,256,128]{2,1,0:T(8,128)(2,1)S(1)}, f32[64,8192]{1,0:T(8,128)S(1)}) custom-call(s32[64]{0:T(128)} %pos_ref.1, bf16[64,8192]{1,0:T(8,128)(2,1)} %h_hbm.1, bf16[64,128]{1,0:T(8,128)(2,1)} %bitcast.9, s32[1,64]{1,0:T(1,128)} %bitcast.6, bf16[8192,2560]{1,0:T(8,128)(2,1)} %w_ref.1, ...), custom_call_target="tpu_custom_call" | custom-call | tf_op jit(solution)/shard_map/main/pallas_call | solution.py:501
  45.0 0.0 copy-done
  45.0 4.5 %write.1 = (bf16[64,8192]{1,0:T(8,128)(2,1)}, bf16[64,256,128]{2,1,0:T(8,128)(2,1)}, bf16[64,256,128]{2,1,0:T(8,128)(2,1)}, bf16[64,256,128]{2,1,0:T(8,128)(2,1)S(1)}, bf16[64,256,128]{2,1,0:T(8,128)(2,1)S(1)}) custom-call(s32[64]{0:T(128)S(1)} %copy-done, ...), custom_call_target="tpu_custom_call", output_to_operand_aliasing={{3}: (3, {}), {4}: (4, {})} | custom-call | tf_op jit(solution)/shard_map/write/pallas_call | solution.py:542
Async XLA Ops:
  0.6 44.3 %copy-start = (s32[64]{0:T(128)S(1)}, s32[64]{0:T(128)}, u32[]{:S(2)}) copy-start(s32[64]{0:T(128)} %pos_ref.1) | copy-start | bytes 772
